TPU v7x, 32 devices: a 4x4x1 block of a 4x4x8 slice. The times are simulated.
32 devices in a mesh: dp: 1 (over z), tp: 4 (over y), sp: 8 (over x, core).
Axes of the slice: x: 4, y: 4, z: 1, core: 2. Of those that a mesh axis runs over, the one named last changes fastest.
The devices are a block of a 4x4x8 slice.
Arguments:
- x_in: bfloat16 [128, 6144], P('dp')
- positions: int32 [128], P('dp')
- k_cache: bfloat16 [128, 512, 8, 128], P('dp', 'sp', 'tp')
- v_cache: bfloat16 [128, 512, 8, 128], P('dp', 'sp', 'tp')
- attn_gain: bfloat16 [6144], replicated
- w_q: bfloat16 [6144, 6144], P(None, 'tp')
- w_k: bfloat16 [6144, 1024], P(None, 'tp')
- w_v: bfloat16 [6144, 1024], P(None, 'tp')
- w_o: bfloat16 [6144, 6144], P('tp')
- mlp_gain: bfloat16 [6144], replicated
- w_gate: bfloat16 [6144, 16384], P(None, ('tp', 'sp'))
- w_up: bfloat16 [6144, 16384], P(None, ('tp', 'sp'))
- w_down: bfloat16 [16384, 6144], P(('tp', 'sp'))
Outputs:
- output 1: bfloat16 [128, 6144], P('dp')
- output 2: bfloat16 [128, 512, 8, 128], P('dp', 'sp', 'tp')
- output 3: bfloat16 [128, 512, 8, 128], P('dp', 'sp', 'tp')
- output 4: bfloat16 [128, 8, 128], P('dp', 'tp')
- output 5: bfloat16 [128, 8, 128], P('dp', 'tp')
All inputs are finite; a program needn't handle non-finite values.
Results may differ from a plain program's by a relative error of at most 0.016995.
Values sent between devices are 32-bit elements.
A program may use at most 768 MiB of HBM per device.

v0:
```python
import jax
import jax.numpy as jnp
from jax import lax
from jax.sharding import PartitionSpec as P

ROPE_THETA = 1000000.0
NORM_EPS = 1e-05
MASK_FILL = -1.0e30


def rms_norm(row_vals, gain_vec):
    vals32 = row_vals.astype(jnp.float32)
    inv_rms = lax.rsqrt(jnp.mean(vals32 * vals32, axis=-1, keepdims=True) + NORM_EPS)
    return (vals32 * inv_rms * gain_vec.astype(jnp.float32)).astype(jnp.bfloat16)


def apply_rotary(head_vecs, positions):
    head_dim = head_vecs.shape[-1]
    half_dim = head_dim // 2
    inv_freq = ROPE_THETA ** (jnp.arange(half_dim, dtype=jnp.float32) * (-2.0 / head_dim))
    angles = positions.astype(jnp.float32)[:, None] * inv_freq[None, :]
    cos_part = jnp.cos(angles)[:, None, :]
    sin_part = jnp.sin(angles)[:, None, :]
    lower_half = head_vecs[..., :half_dim]
    upper_half = head_vecs[..., half_dim:]
    return jnp.concatenate([lower_half * cos_part - upper_half * sin_part, upper_half * cos_part + lower_half * sin_part], axis=-1)


def solution(mesh):
    row_spec = P('dp', None)
    cache_spec = P('dp', 'sp', 'tp', None)
    new_spec = P('dp', 'tp', None)
    in_specs = (row_spec, P('dp'), cache_spec, cache_spec, P(None), P(None, 'tp'), P(None, 'tp'), P(None, 'tp'), P('tp', None), P(None), P(None, ('tp', 'sp')), P(None, ('tp', 'sp')), P(('tp', 'sp'), None))
    out_specs = (row_spec, cache_spec, cache_spec, new_spec, new_spec)

    def local_step(x_in, positions, k_cache, v_cache, attn_gain, w_q, w_k, w_v, w_o, mlp_gain, w_gate, w_up, w_down):
        num_rows, block_len, kv_local, head_dim = k_cache.shape
        heads_local = w_q.shape[1] // head_dim
        group_size = heads_local // kv_local
        normed = rms_norm(x_in, attn_gain)
        q_proj = jnp.dot(normed, w_q, preferred_element_type=jnp.float32).astype(jnp.bfloat16)
        k_proj = jnp.dot(normed, w_k, preferred_element_type=jnp.float32).astype(jnp.bfloat16)
        v_new = jnp.dot(normed, w_v, preferred_element_type=jnp.float32).astype(jnp.bfloat16).reshape(num_rows, kv_local, head_dim)
        q_rot = apply_rotary(q_proj.astype(jnp.float32).reshape(num_rows, heads_local, head_dim), positions).astype(jnp.bfloat16)
        k_new = apply_rotary(k_proj.astype(jnp.float32).reshape(num_rows, kv_local, head_dim), positions).astype(jnp.bfloat16)
        slot_ids = lax.axis_index('sp') * block_len + jnp.arange(block_len)
        slot_hit = (slot_ids[None, :] == positions[:, None])[:, :, None, None]
        k_out = jnp.where(slot_hit, k_new[:, None], k_cache)
        v_out = jnp.where(slot_hit, v_new[:, None], v_cache)
        q_grouped = q_rot.reshape(num_rows, kv_local, group_size, head_dim)
        scores = jnp.einsum('bkgd,btkd->bkgt', q_grouped, k_out, preferred_element_type=jnp.float32) * (head_dim ** -0.5)
        is_valid = (slot_ids[None, :] <= positions[:, None])[:, None, None, :]
        scores = jnp.where(is_valid, scores, MASK_FILL)
        local_max = jnp.max(scores, axis=-1)
        weights = jnp.where(is_valid, jnp.exp(scores - local_max[..., None]), 0.0)
        local_sum = jnp.sum(weights, axis=-1)
        local_num = jnp.einsum('bkgt,btkd->bkgd', weights.astype(jnp.bfloat16), v_out, preferred_element_type=jnp.float32)
        global_max = lax.pmax(local_max, 'sp')
        rescale = jnp.exp(local_max - global_max)
        packed = jnp.concatenate([local_num * rescale[..., None], (local_sum * rescale)[..., None]], axis=-1)
        merged = lax.psum(packed, 'sp')
        attn_out = (merged[..., :head_dim] / merged[..., head_dim:]).astype(jnp.bfloat16).reshape(num_rows, heads_local * head_dim)
        attn_part = jnp.dot(attn_out, w_o, preferred_element_type=jnp.float32)
        attn_sum = lax.psum(attn_part, 'tp')
        x_mid = (x_in.astype(jnp.float32) + attn_sum).astype(jnp.bfloat16)
        normed_mlp = rms_norm(x_mid, mlp_gain)
        gate_val = jnp.dot(normed_mlp, w_gate, preferred_element_type=jnp.float32)
        up_val = jnp.dot(normed_mlp, w_up, preferred_element_type=jnp.float32)
        inner_act = (jax.nn.silu(gate_val) * up_val).astype(jnp.bfloat16)
        mlp_part = jnp.dot(inner_act, w_down, preferred_element_type=jnp.float32)
        mlp_sum = lax.psum(mlp_part, ('tp', 'sp'))
        x_out = (x_mid.astype(jnp.float32) + mlp_sum).astype(jnp.bfloat16)
        return x_out, k_out, v_out, k_new, v_new

    return jax.shard_map(local_step, mesh=mesh, in_specs=in_specs, out_specs=out_specs, check_vma=False)
```

profile of v0, /device:TPU:97, one launch (start us, length us, event | category | flops | bytes accessed | tf_op | source)
XLA Modules:
  0.0 357.0 jit_solution(6608629764532085651)
XLA Ops:
  7.2 0.0 copy-start
  7.2 0.1 all-reduce.4.cloned.1.call-start
  7.3 0.8 convert_element_type.61
  8.1 1.8 fusion.4
  10.0 0.7 convert_element_type.58
  10.7 1.3 broadcast_compare_fusion.1
  12.0 0.2 multiply_cosine_fusion
  12.2 0.7 copy.49
  12.9 0.7 copy.50
  13.7 0.0 copy-done
  13.7 2.0 convolution_convert_fusion.1
  15.7 0.0 copy-start.2
  15.7 0.7 broadcast_in_dim.73
  16.4 3.0 fusion.23
  19.4 0.1 reshape.178
  19.5 0.0 copy-done.2
  19.5 7.8 %fusion.12 = f32[128,1536]{1,0:T(8,128)S(1)} fusion(bf16[6144,1536]{1,0:T(8,128)(2,1)} %param.18, bf16[128,6144]{1,0:T(8,128)(2,1)S(1)} %copy-done.2, f32[6144]{0:T(1024)S(1)} %convert_element_type.58, f32[128]{0:T(128)S(1)} %add_rsqrt_fusion.1), kind=kOutput, calls=%fused_computation.21 | convolution fusion | flops 2419458048 | bytes 21258752 | tf_op jit(solution)/shard_map/dot_general | solution.py:41
  27.3 0.3 copy.46
  27.6 0.0 copy-start.8
  27.6 0.1 subtract_convert_fusion
  27.7 0.4 copy.48
  28.2 1.2 copy.47
  29.3 1.1 subtract_convert_fusion.1
  30.4 0.2 pad_maximum_fusion.1
  30.6 0.0 copy-start.7
  30.7 0.0 copy-done.8
  30.7 0.0 copy-start.6
  30.7 14.9 %broadcast_select_fusion = (bf16[128,64,2,128]{3,2,1,0:T(2,128)(2,1)}, bf16[128,64,2,128]{3,2,1,0:T(2,128)(2,1)S(1)}) fusion(bf16[128,64,2,128]{3,2,1,0:T(2,128)(2,1)} %param.16, pred[128,64]{1,0:T(8,128)(4,1)} %get-tuple-element.16, bf16[128,2,128]{2,1,0:T(2,128)(2,1)S(1)} %copy-done.8, bf16[128,64,2,128]{3,2,1,0:T(2,128)(2,1)} %param.15, ...), kind=kLoop, calls=%fused_computation | loop fusion | flops 4194304 | bytes 16916480 | tf_op jit(solution)/shard_map/jit(_where)/select_n | solution.py:49
  45.6 0.0 copy-done.7
  45.6 0.0 copy-start.3
  45.6 0.0 copy-done.6
  45.6 2.7 fusion.52
  48.3 0.0 copy-done.3
  48.3 25.3 %pmax.7 = f32[128,2,6]{2,1,0:T(2,128)S(1)} all-reduce(f32[128,2,6]{2,1,0:T(2,128)S(1)} %get-tuple-element.19), channel_id=1, replica_groups=mesh['dp'=1,'tp'=4,'sp'=8] {'sp'}, use_global_device_ids=true, to_apply=%region_2.3 | all-reduce | flops 1536 | bytes 12288 | tf_op jit(solution)/shard_map/pmax | solution.py:58
  73.6 0.8 fusion.26
  74.4 0.1 multiply_bitcast_fusion
  74.6 2.6 copy.54
  77.1 0.0 copy-start.5
  77.2 3.7 %fusion.19 = f32[128,2,6,128]{3,2,1,0:T(8,128)S(1)} fusion(bf16[128,64,2,128]{3,2,1,0:T(2,128)(2,1)} %get-tuple-element.13, f32[128,2,6,64]{3,2,1,0:T(8,128)S(1)} %get-tuple-element.20, f32[128,2,6]{2,1,0:T(2,128)S(1)} %get-tuple-element.8, f32[128,2,6]{2,1,0:T(2,128)S(1)} %get-tuple-element.19, pred[128,64]{1,0:T(8,128)(4,1)S(1)} %get-tuple-element.15), kind=kOutput, calls=%fused_computation.25 | convolution fusion | flops 25657344 | bytes 5394432 | tf_op jit(solution)/shard_map/bkgt,btkd->bkgd/dot_general | solution.py:57
  80.8 0.0 copy-done.5
  80.8 1.6 pad_maximum_fusion
  82.4 0.1 all-reduce.4.cloned.1.call-update
  82.5 0.2 all-reduce.6.cloned.1.call-start
  82.7 61.7 %all-reduce.4.cloned.1.call-done = f32[128,2,6,129]{3,2,1,0:T(8,128)} async-done(((f32[128,2,6,129]{3,2,1,0:T(8,128)}), f32[128,2,6,129]{3,2,1,0:T(8,128)}) %all-reduce.4.cloned.1.call-update) | async-done | bytes 792592 | tf_op jit(solution)/shard_map/psum | solution.py:61
  144.4 1.3 slice.29
  145.7 1.7 copy.60
  147.4 1.6 fusion.24
  149.0 0.4 copy.57
  149.4 10.8 %fusion.53 = f32[128,6144]{1,0:T(8,128)} fusion(bf16[128,1536]{0,1:T(8,128)(2,1)S(1)} %bitcast.17, bf16[1536,6144]{1,0:T(8,128)(2,1)} %param.21), kind=kOutput, calls=%fused_computation.69 | convolution fusion | flops 2415919104 | bytes 22413312 | tf_op jit(solution)/shard_map/dot_general | solution.py:63
  160.1 0.0 copy-start.9
  160.1 0.1 all-reduce.6.cloned.1.call-update
  160.2 0.1 all-reduce.8.cloned.1.call-start
  160.2 0.6 copy-done.9
  160.8 71.2 %all-reduce.6.cloned.1.call-done = f32[128,6144]{1,0:T(8,128)} async-done(((f32[128,6144]{1,0:T(8,128)}), f32[128,6144]{1,0:T(8,128)}) %all-reduce.6.cloned.1.call-update) | async-done | bytes 3145744 | tf_op jit(solution)/shard_map/psum | solution.py:64
  232.1 2.4 fusion.8
  234.5 0.0 copy-start.4
  234.5 4.4 %fusion.37 = f32[128,512]{1,0:T(8,128)S(1)} fusion(bf16[6144,512]{1,0:T(8,128)(2,1)} %param.23, bf16[128,6144]{1,0:T(8,128)(2,1)S(1)} %get-tuple-element.6, f32[6144]{0:T(1024)S(1)} %convert_element_type.68, f32[128]{0:T(128)S(1)} %add_rsqrt_fusion), kind=kOutput, calls=%fused_computation.43 | convolution fusion | flops 808452096 | bytes 8151552 | tf_op jit(solution)/shard_map/dot_general | solution.py:67
  238.9 0.0 copy-done.4
  238.9 8.2 %fusion.25 = f32[128,6144]{1,0:T(8,128)} fusion(bf16[512,6144]{1,0:T(8,128)(2,1)} %param.25, bf16[6144,512]{1,0:T(8,128)(2,1)} %param.24, bf16[128,6144]{1,0:T(8,128)(2,1)S(1)} %get-tuple-element.6, f32[6144]{0:T(1024)S(1)} %convert_element_type.68, f32[128]{0:T(128)S(1)} %add_rsqrt_fusion, f32[128,512]{1,0:T(8,128)S(1)} %fusion.37), kind=kOutput, calls=%fused_computation.34 | convolution fusion | flops 1614151680 | bytes 17588736 | tf_op jit(solution)/shard_map/dot_general | solution.py:70
  247.2 0.1 all-reduce.8.cloned.1.call-update
  247.2 0.0 copy-start.1
  247.2 99.5 %all-reduce.8.cloned.1.call-done = f32[128,6144]{1,0:T(8,128)} async-done(((f32[128,6144]{1,0:T(8,128)}), f32[128,6144]{1,0:T(8,128)}) %all-reduce.8.cloned.1.call-update) | async-done | bytes 3145744 | tf_op jit(solution)/shard_map/psum | solution.py:71
  346.7 3.8 %fusion.11 = bf16[128,6144]{1,0:T(8,128)(2,1)} fusion(f32[128,6144]{1,0:T(8,128)} %all-reduce.8.cloned.1.call-done, bf16[128,6144]{1,0:T(8,128)(2,1)} %copy-done.4), kind=kLoop, calls=%fused_computation.19 | loop fusion | flops 2359296 | bytes 6291456 | tf_op jit(solution)/shard_map/convert_element_type | solution.py:72
  350.5 0.0 copy-done.1
  (5 shorter events, 0.0 us)
Async XLA Ops:
  7.2 6.5 %copy-start = (bf16[6144,256]{1,0:T(8,128)(2,1)S(1)}, bf16[6144,256]{1,0:T(8,128)(2,1)}, u32[]{:S(2)}) copy-start(bf16[6144,256]{1,0:T(8,128)(2,1)} %param.20) | copy-start | bytes 9437188
  7.2 137.2 %all-reduce.4.cloned.1.call-start = ((), (), s32[]{:S(2)}) async-start(), calls=%async_computation | async-start | bytes 4194304 | tf_op jit(solution)/shard_map/psum | solution.py:61
  15.7 3.7 %copy-start.2 = (bf16[128,6144]{1,0:T(8,128)(2,1)S(1)}, bf16[128,6144]{1,0:T(8,128)(2,1)}, u32[]{:S(2)}) copy-start(bf16[128,6144]{1,0:T(8,128)(2,1)} %param.13) | copy-start | bytes 4718596
  27.6 3.1 copy-start.8
  30.6 15.0 %copy-start.7 = (bf16[128,2,128]{2,1,0:T(2,128)(2,1)}, bf16[128,2,128]{2,1,0:T(2,128)(2,1)S(1)}, u32[]{:S(2)}) copy-start(bf16[128,2,128]{2,1,0:T(2,128)(2,1)S(1)} %pad_maximum_fusion.1) | copy-start | bytes 196612
  30.7 15.0 %copy-start.6 = (bf16[128,2,6,64]{3,2,1,0:T(8,128)(2,1)S(1)}, bf16[128,2,6,64]{3,2,1,0:T(8,128)(2,1)}, u32[]{:S(2)}) copy-start(bf16[128,2,6,64]{3,2,1,0:T(8,128)(2,1)} %copy.47) | copy-start | bytes 589828
  45.6 2.7 copy-start.3
  77.1 3.7 %copy-start.5 = (f32[128,2,6,1]{3,2,1,0:T(8,128)S(1)}, f32[128,2,6,1]{3,2,1,0:T(8,128)}, u32[]{:S(2)}) copy-start(f32[128,2,6,1]{3,2,1,0:T(8,128)} %copy.54) | copy-start | bytes 18436
  82.5 149.6 %all-reduce.6.cloned.1.call-start = ((), (), s32[]{:S(2)}) async-start(), calls=%async_computation.1 | async-start | bytes 6291456 | tf_op jit(solution)/shard_map/psum | solution.py:64
  160.1 0.7 copy-start.9
  160.2 186.5 %all-reduce.8.cloned.1.call-start = ((), (), s32[]{:S(2)}) async-start(), calls=%async_computation.2 | async-start | bytes 6291456 | tf_op jit(solution)/shard_map/psum | solution.py:71
  234.5 4.4 %copy-start.4 = (bf16[128,6144]{1,0:T(8,128)(2,1)}, bf16[128,6144]{1,0:T(8,128)(2,1)S(1)}, u32[]{:S(2)}) copy-start(bf16[128,6144]{1,0:T(8,128)(2,1)S(1)} %get-tuple-element.6) | copy-start | bytes 4718596
  247.2 103.3 %copy-start.1 = (bf16[6144,256]{1,0:T(8,128)(2,1)S(1)}, bf16[6144,256]{1,0:T(8,128)(2,1)}, u32[]{:S(2)}) copy-start(bf16[6144,256]{1,0:T(8,128)(2,1)} %param.20) | copy-start | bytes 9437188
Sparse Core Ops, SparseCore 0:
  82.6 61.7 all-reduce.3
  160.3 71.7 all-reduce.5
  247.3 99.2 all-reduce.7
where the time goes:
time: 358 us; the launch traced here: 357 us
  waiting for transfers between devices  233 us (65%)
  matrix products  42.6 us (12%)
  other arithmetic  31.6 us (9%)
  blocking collectives  25.3 us (7%)
  between operations  14.1 us (4%)
  local copies, waits for them, and re-layouts  10.6 us (3%)
    psum x1, waiting for transfers between devices, local_step(): mlp_sum = lax.psum(mlp_part, ('tp', 'sp'))  99.5 us
    psum x1, waiting for transfers between devices, local_step(): attn_sum = lax.psum(attn_part, 'tp')  71.2 us
    psum x1, waiting for transfers between devices, local_step(): merged = lax.psum(packed, 'sp')  61.7 us
    pmax x1, blocking collectives, local_step(): global_max = lax.pmax(local_max, 'sp')  25.3 us
    select_n x1, other arithmetic, local_step(): v_out = jnp.where(slot_hit, v_new[:, None], v_cache)  14.9 us
    dot_general x1, matrix products, local_step(): attn_part = jnp.dot(attn_out, w_o, preferred_element_type=jnp.float32)  10.8 us
    dot_general x1, matrix products, local_step(): mlp_part = jnp.dot(inner_act, w_down, preferred_element_type=jnp.float32)  8.23 us
    dot_general x1, matrix products, local_step(): jnp.dot(normed, w_q, preferred_element_type=jnp.float32)  7.84 us
  transfers between devices with their start and end apart: 3, of which 3 were waited for; matrix products, arithmetic and copies ran while one was open for 0% of the time, Pallas kernels for 0%

commit v1 on v0

v1 whole, which is shorter than its diff:
```python
import functools

import jax
import jax.numpy as jnp
from jax import lax
from jax.experimental import pallas as pl
from jax.experimental.pallas import tpu as pltpu
from jax.sharding import PartitionSpec as P

ROPE_THETA = 1000000.0
NORM_EPS = 1e-05
MASK_FILL = -1.0e30
LANES = 128
SUBROWS = 8
CORES = 2
TILE = 512
MESH = pl.DeviceIdType.MESH
F32 = jnp.float32
BF16 = jnp.bfloat16


def rms_norm(row_vals, gain_vec):
    vals32 = row_vals.astype(F32)
    inv_rms = lax.rsqrt(jnp.mean(vals32 * vals32, axis=-1, keepdims=True) + NORM_EPS)
    return (vals32 * inv_rms * gain_vec.astype(F32)).astype(BF16)


def rotary_tables(positions, head_dim):
    half_dim = head_dim // 2
    inv_freq = ROPE_THETA ** (jnp.arange(half_dim, dtype=F32) * (-2.0 / head_dim))
    angles = positions.astype(F32)[:, None] * inv_freq[None, :]
    return jnp.cos(angles), jnp.sin(angles)


def apply_rotary(head_vecs, cos_part, sin_part):
    half_dim = head_vecs.shape[-1] // 2
    cos_part, sin_part = cos_part[:, None, :], sin_part[:, None, :]
    lower_half = head_vecs[..., :half_dim]
    upper_half = head_vecs[..., half_dim:]
    return jnp.concatenate([lower_half * cos_part - upper_half * sin_part, upper_half * cos_part + lower_half * sin_part], axis=-1)


def run_together(*flows):
    flows = list(flows)
    while flows:
        for flow in list(flows):
            if next(flow, flow) is flow:
                flows.remove(flow)


def merge_partials(left, right):
    width = left.shape[-1] - LANES
    stat_l, stat_r = left[:, width:], right[:, width:]
    lane = lax.broadcasted_iota(jnp.int32, stat_l.shape, 1)
    top = jnp.maximum(stat_l, stat_r)
    scale_l, scale_r = jnp.exp(stat_l - top), jnp.exp(stat_r - top)
    total = stat_l * pltpu.roll(scale_l, LANES // 2, 1) + stat_r * pltpu.roll(scale_r, LANES // 2, 1)
    parts = []
    for g in range(width // LANES):
        cols = slice(g * LANES, (g + 1) * LANES)
        parts.append(left[:, cols] * scale_l[:, g : g + 1] + right[:, cols] * scale_r[:, g : g + 1])
    parts.append(jnp.where(lane < LANES // 2, top, total))
    return jnp.concatenate(parts, axis=-1)


def rest_kernel(
    nx, ny, dim,
    part_ref, own_x_ref, gain_ref, wo_hbm, w1_hbm, w3_hbm, w2_hbm,
    out_ref,
    wo_v, w1_v, w3_v, w2_v, load_sem,
    pair_in, ring_a, ring_a_in, o_in, proj, proj_in, stat_out, stat_in,
    gathered, normed, other, other_in, mine, big_in, small_in, final,
    send_sem, recv_sem,
):
    sp, iy = lax.axis_index("sp"), lax.axis_index("tp")
    ix, core = sp // CORES, lax.rem(sp, CORES)
    half = wo_v.shape[1]
    heads_width = part_ref.shape[-1] - LANES

    def on_x(step):
        return lax.rem(ix + step + nx, nx)

    def on_y(step):
        return lax.rem(iy + step + ny, ny)

    partner = {"sp": ix * CORES + (1 - core)}
    x_right, x_left = {"sp": on_x(1) * CORES + core}, {"sp": on_x(-1) * CORES + core}
    y_right, y_left = {"tp": on_y(1)}, {"tp": on_y(-1)}

    loads = []

    def load(src, dst):
        copy = pltpu.make_async_copy(src, dst, load_sem.at[len(loads)])
        copy.start()
        loads.append(copy)
        return copy

    my_cols = pl.ds(pl.multiple_of(core * half, half), half)
    wo_load = load(wo_hbm.at[:, my_cols], wo_v)
    w1_load = load(w1_hbm, w1_v)
    w3_load = load(w3_hbm, w3_v)
    w2_load = load(w2_hbm, w2_v)

    barrier = pltpu.get_barrier_semaphore()
    peers = (partner, x_right, x_left, y_right, y_left)
    for peer in peers:
        pl.semaphore_signal(barrier, inc=1, device_id=peer, device_id_type=MESH)
    pl.semaphore_wait(barrier, len(peers))

    sent = []

    def send(src, dst, peer):
        k = len(sent)
        copy = pltpu.make_async_remote_copy(
            src_ref=src, dst_ref=dst, send_sem=send_sem.at[k], recv_sem=recv_sem.at[k], device_id=peer, device_id_type=MESH
        )
        copy.start()
        sent.append(copy)
        return copy

    def ring_reduce(piece, held, at, right, left, add, done):
        near_r, near_l, far = at(1), at(-1), at(2)
        r1 = send(piece(far, 0), held.at[0], right)
        l1 = send(piece(far, 1), held.at[1], left)
        r2 = send(piece(near_r, 1), held.at[2], right)
        l2 = send(piece(near_l, 0), held.at[3], left)
        yield
        r1.wait_recv()
        add(piece(near_r, 0), held.at[0])
        r3 = send(piece(near_r, 0), held.at[4], right)
        l1.wait_recv()
        add(piece(near_l, 1), held.at[1])
        l3 = send(piece(near_l, 1), held.at[5], left)
        yield
        me = at(0)
        l2.wait_recv()
        add(piece(me, 0), held.at[3])
        r2.wait_recv()
        add(piece(me, 1), held.at[2])
        yield
        r3.wait_recv()
        add(piece(me, 0), held.at[4])
        l3.wait_recv()
        add(piece(me, 1), held.at[5])
        done()

    def ring_gather(piece, at, right, left, arrived):
        me, from_l, from_r, far = at(0), at(-1), at(1), at(2)
        r1 = send(piece(me, 0), piece(me, 0), right)
        l1 = send(piece(me, 1), piece(me, 1), left)
        r2 = send(piece(me, 1), piece(me, 1), right)
        l2 = send(piece(me, 0), piece(me, 0), left)
        yield
        r1.wait_recv()
        r3 = send(piece(from_l, 0), piece(from_l, 0), right)
        arrived(piece(from_l, 0))
        l1.wait_recv()
        l3 = send(piece(from_r, 1), piece(from_r, 1), left)
        arrived(piece(from_r, 1))
        yield
        r2.wait_recv()
        arrived(piece(from_l, 1))
        l2.wait_recv()
        arrived(piece(from_r, 0))
        yield
        r3.wait_recv()
        arrived(piece(far, 0))
        l3.wait_recv()
        arrived(piece(far, 1))

    def add_into(dst, src):
        dst[...] = dst[...] + src[...]

    order = (on_x(2), on_x(1), on_x(-1), on_x(0))
    swaps = [send(part_ref.at[1 - core, t], pair_in.at[t], partner) for t in order]
    for t, swap in zip(order, swaps):
        swap.wait_recv()
        ring_a[t] = merge_partials(part_ref[core, t], pair_in[t])

    rows_half = ring_a.shape[1] // 2

    def part_piece(t, h):
        return ring_a.at[t, pl.ds(h * rows_half, rows_half)]

    def merge_into(dst, src):
        dst[...] = merge_partials(dst[...], src[...])

    run_together(ring_reduce(part_piece, ring_a_in, on_x, x_right, x_left, merge_into, lambda: None))
    merged = ring_a[on_x(0)]
    stats = merged[:, heads_width:]
    heads = []
    for g in range(heads_width // LANES):
        lsum = stats[:, LANES // 2 + g : LANES // 2 + g + 1]
        heads.append(merged[:, g * LANES : (g + 1) * LANES] / lsum)
    o_in[core] = jnp.concatenate(heads, axis=-1).astype(BF16).astype(F32)
    swap = send(o_in.at[core], o_in.at[core], partner)
    swap.wait_recv()
    attn = jnp.concatenate([o_in[c] for c in range(CORES)], axis=-1).astype(BF16)

    wo_load.wait()
    tiles = half // TILE
    for j in range(tiles):
        cols = slice(j * TILE, (j + 1) * TILE)
        prod = jnp.dot(attn, wo_v[:, cols], preferred_element_type=F32)
        proj[:, :, cols] = prod.reshape(ny, SUBROWS, TILE)

    def proj_piece(t, h):
        return proj.at[t, :, pl.ds(h * (half // 2), half // 2)]

    run_together(ring_reduce(proj_piece, proj_in, on_y, y_right, y_left, add_into, lambda: None))
    x_mid = (own_x_ref[...] + proj[iy]).astype(BF16).astype(F32)

    square = jnp.sum(x_mid * x_mid, axis=-1, keepdims=True)
    stat_out[...] = jnp.broadcast_to(square, stat_out.shape)
    swap = send(stat_out, stat_in, partner)
    swap.wait_recv()
    inv_rms = lax.rsqrt((stat_out[:, :1] + stat_in[:, :1]) / dim + NORM_EPS)
    gathered[core, ix, iy] = (x_mid * inv_rms * gain_ref[core]).astype(BF16).astype(F32)

    def gather_all(buf):
        quarter, eighth = half // 2, half // 4
        forwards = []

        def forward(ref_of):
            ref = ref_of(core)
            forwards.append(send(ref, ref, partner))

        def at(*index):
            return lambda c: buf.at[(c, *index)]

        forward(at(ix, iy))

        def flow(lo, y_first):
            def cols(h):
                return pl.ds(lo + h * eighth, eighth)

            def along_y_one(t, h):
                return buf.at[core, ix, t, :, cols(h)]

            def along_x_one(t, h):
                return buf.at[core, t, iy, :, cols(h)]

            def along_x_all(t, h):
                return buf.at[core, t, :, :, cols(h)]

            def along_y_all(t, h):
                return buf.at[core, :, t, :, cols(h)]

            def arrived(ref):
                forwards.append(send(ref, ref, partner))

            if y_first:
                yield from ring_gather(along_y_one, on_y, y_right, y_left, arrived)
                yield from ring_gather(along_x_all, on_x, x_right, x_left, arrived)
            else:
                yield from ring_gather(along_x_one, on_x, x_right, x_left, arrived)
                yield from ring_gather(along_y_all, on_y, y_right, y_left, arrived)

        run_together(flow(0, True), flow(quarter, False))
        for copy in forwards:
            copy.wait_recv()

    gather_all(gathered)
    rows = nx * ny * SUBROWS
    for c in range(CORES):
        normed[:, c * half : (c + 1) * half] = gathered[c].reshape(rows, half).astype(BF16)

    w1_load.wait()
    w3_load.wait()
    inner = w1_v.shape[1]
    step = 256
    acts = []
    for j in range(inner // step):
        cols = slice(j * step, (j + 1) * step)
        gate = jnp.dot(normed[...], w1_v[:, cols], preferred_element_type=F32)
        up = jnp.dot(normed[...], w3_v[:, cols], preferred_element_type=F32)
        acts.append((gate * jax.nn.sigmoid(gate) * up).astype(BF16))
    act = jnp.concatenate(acts, axis=-1)
    w2_load.wait()

    def down(which, j):
        cols = pl.ds(pl.multiple_of(which * half + j * TILE, TILE), TILE)
        return jnp.dot(act, w2_v[:, cols], preferred_element_type=F32).reshape(nx, ny, SUBROWS, TILE)

    swaps = []
    for j in range(tiles):
        cols = slice(j * TILE, (j + 1) * TILE)
        other[:, :, :, cols] = down(1 - core, j)
        swaps.append(send(other.at[:, :, :, cols], other_in.at[:, :, :, cols], partner))

    quarter, eighth = half // 2, half // 4

    def reduce_flow(index):
        lo = index * quarter

        def along_x_all(t, h):
            return mine.at[t, :, :, pl.ds(lo + h * eighth, eighth)]

        def along_y_all(t, h):
            return mine.at[:, t, :, pl.ds(lo + h * eighth, eighth)]

        def along_y_one(t, h):
            return mine.at[ix, t, :, pl.ds(lo + h * eighth, eighth)]

        def along_x_one(t, h):
            return mine.at[t, iy, :, pl.ds(lo + h * eighth, eighth)]

        for j in range(index * tiles // 2, (index + 1) * tiles // 2):
            cols = slice(j * TILE, (j + 1) * TILE)
            swaps[j].wait_recv()
            mine[:, :, :, cols] = down(core, j) + other_in[:, :, :, cols]
        if index == 0:
            yield from ring_reduce(along_x_all, big_in.at[0], on_x, x_right, x_left, add_into, lambda: None)
            yield from ring_reduce(along_y_one, small_in.at[0], on_y, y_right, y_left, add_into, lambda: None)
        else:
            yield from ring_reduce(along_y_all, big_in.at[1], on_y, y_right, y_left, add_into, lambda: None)
            yield from ring_reduce(along_x_one, small_in.at[1], on_x, x_right, x_left, add_into, lambda: None)

    run_together(reduce_flow(0), reduce_flow(1))
    final[core, ix, iy] = (x_mid + mine[ix, iy]).astype(BF16).astype(F32)
    gather_all(final)
    for c in range(CORES):
        out_ref[:, c * half : (c + 1) * half] = final[c].reshape(rows, half).astype(BF16)
    for copy in sent:
        copy.wait_send()


def rest_of_layer(mesh, parts, own_x, gain, w_o, w_gate, w_up, w_down):
    nx, ny = mesh.shape["sp"] // CORES, mesh.shape["tp"]
    dim = w_o.shape[1]
    half = dim // CORES
    rows = nx * ny * SUBROWS
    heads_width = parts.shape[-1] - LANES
    eighth = half // 4
    any_spec = pl.BlockSpec(memory_space=pltpu.HBM)
    vmem_spec = pl.BlockSpec(memory_space=pltpu.VMEM)
    width = heads_width + LANES
    chunk_rows = ny * SUBROWS
    count = 152
    scratch = [
        pltpu.VMEM((w_o.shape[0], half), BF16),
        pltpu.VMEM(w_gate.shape, BF16),
        pltpu.VMEM(w_up.shape, BF16),
        pltpu.VMEM(w_down.shape, BF16),
        pltpu.SemaphoreType.DMA((4,)),
        pltpu.VMEM((nx, chunk_rows, width), F32),
        pltpu.VMEM((nx, chunk_rows, width), F32),
        pltpu.VMEM((6, chunk_rows // 2, width), F32),
        pltpu.VMEM((CORES, chunk_rows, heads_width), F32),
        pltpu.VMEM((ny, SUBROWS, half), F32),
        pltpu.VMEM((6, SUBROWS, half // 2), F32),
        pltpu.VMEM((SUBROWS, LANES), F32),
        pltpu.VMEM((SUBROWS, LANES), F32),
        pltpu.VMEM((CORES, nx, ny, SUBROWS, half), F32),
        pltpu.VMEM((rows, dim), BF16),
        pltpu.VMEM((nx, ny, SUBROWS, half), F32),
        pltpu.VMEM((nx, ny, SUBROWS, half), F32),
        pltpu.VMEM((nx, ny, SUBROWS, half), F32),
        pltpu.VMEM((2, 6, nx, SUBROWS, eighth), F32),
        pltpu.VMEM((2, 6, SUBROWS, eighth), F32),
        pltpu.VMEM((CORES, nx, ny, SUBROWS, half), F32),
        pltpu.SemaphoreType.DMA((count,)),
        pltpu.SemaphoreType.DMA((count,)),
    ]
    return pl.pallas_call(
        functools.partial(rest_kernel, nx, ny, dim),
        out_shape=jax.ShapeDtypeStruct((rows, dim), BF16),
        in_specs=[vmem_spec] * 3 + [any_spec] * 4,
        out_specs=vmem_spec,
        scratch_shapes=scratch,
        compiler_params=pltpu.CompilerParams(collective_id=0, has_side_effects=True, vmem_limit_bytes=60 * 1024 * 1024),
        name="rest_of_layer",
    )(parts, own_x, gain, w_o, w_gate, w_up, w_down)


def solution(mesh):
    row_spec = P('dp', None)
    cache_spec = P('dp', 'sp', 'tp', None)
    new_spec = P('dp', 'tp', None)
    in_specs = (row_spec, P('dp'), cache_spec, cache_spec, P(None), P(None, 'tp'), P(None, 'tp'), P(None, 'tp'), P('tp', None), P(None), P(None, ('tp', 'sp')), P(None, ('tp', 'sp')), P(('tp', 'sp'), None))
    out_specs = (row_spec, cache_spec, cache_spec, new_spec, new_spec)
    nx, ny = mesh.shape["sp"] // CORES, mesh.shape["tp"]

    def local_step(x_in, positions, k_cache, v_cache, attn_gain, w_q, w_k, w_v, w_o, mlp_gain, w_gate, w_up, w_down):
        num_rows, block_len, kv_local, head_dim = k_cache.shape
        dim = x_in.shape[1]
        half = dim // CORES
        heads_local = w_q.shape[1] // head_dim
        group_size = heads_local // kv_local
        normed = rms_norm(x_in, attn_gain)
        q_proj = jnp.dot(normed, w_q, preferred_element_type=F32).astype(BF16)
        k_proj = jnp.dot(normed, w_k, preferred_element_type=F32).astype(BF16)
        v_new = jnp.dot(normed, w_v, preferred_element_type=F32).astype(BF16).reshape(num_rows, kv_local, head_dim)
        cos_part, sin_part = rotary_tables(positions, head_dim)
        q_rot = apply_rotary(q_proj.astype(F32).reshape(num_rows, heads_local, head_dim), cos_part, sin_part).astype(BF16)
        k_new = apply_rotary(k_proj.astype(F32).reshape(num_rows, kv_local, head_dim), cos_part, sin_part).astype(BF16)
        sp = lax.axis_index('sp')
        slot_ids = sp * block_len + jnp.arange(block_len)
        slot_hit = (slot_ids[None, :] == positions[:, None])[:, :, None, None]
        k_out = jnp.where(slot_hit, k_new[:, None], k_cache)
        v_out = jnp.where(slot_hit, v_new[:, None], v_cache)
        q_grouped = q_rot.reshape(num_rows, kv_local, group_size, head_dim)
        scores = jnp.einsum('bkgd,btkd->bkgt', q_grouped, k_out, preferred_element_type=F32) * (head_dim ** -0.5)
        is_valid = (slot_ids[None, :] <= positions[:, None])[:, None, None, :]
        scores = jnp.where(is_valid, scores, MASK_FILL)
        local_max = jnp.max(scores, axis=-1)
        weights = jnp.where(is_valid, jnp.exp(scores - local_max[..., None]), 0.0)
        local_sum = jnp.sum(weights, axis=-1)
        local_num = jnp.einsum('bkgt,btkd->bkgd', weights.astype(BF16), v_out, preferred_element_type=F32)
        gap = ((0, 0), (0, 0), (0, LANES // 2 - group_size))
        parts = jnp.concatenate([local_num.reshape(num_rows, kv_local, group_size * head_dim), jnp.pad(local_max, gap), jnp.pad(local_sum, gap)], axis=-1)
        parts = parts.transpose(1, 0, 2).reshape(kv_local, nx, num_rows // nx, -1)
        row0 = ((sp // CORES) * ny + lax.axis_index('tp')) * SUBROWS
        own_x = lax.dynamic_slice(x_in, (row0, lax.rem(sp, CORES) * half), (SUBROWS, half)).astype(F32)
        gain = mlp_gain.astype(F32).reshape(CORES, 1, half)
        x_out = rest_of_layer(mesh, parts, own_x, gain, w_o, w_gate, w_up, w_down)
        return x_out, k_out, v_out, k_new, v_new

    return jax.shard_map(local_step, mesh=mesh, in_specs=in_specs, out_specs=out_specs, check_vma=False)
```

time: 358 us -> 140 us (0.39)
  waiting for transfers between devices: 233 us -> 0 us
  Pallas kernels: 0 us -> 88.9 us
  blocking collectives: 25.3 us -> 0 us
  matrix products: 42.6 us -> 20.1 us
  between operations: 14.1 us -> 0.88 us
  other arithmetic: 31.6 us -> 22.8 us
  local copies, waits for them, and re-layouts: 10.6 us -> 7.01 us
    psum x3 -> x0, waiting for transfers between devices: 232 us -> none  [the longest x1 99.5 us: local_step(): mlp_sum = lax.psum(mlp_part, ('tp', 'sp'))]
    pallas_call x0 -> x1, Pallas kernels: none -> 88.9 us  [rest_of_layer(): pl.pallas_call(functools.partial(rest_kernel, nx, ny, dim), out_shape=jax...]
    pmax x1 -> x0, blocking collectives: 25.3 us -> none  [local_step(): global_max = lax.pmax(local_max, 'sp')]
    dot_general x8 -> x5, matrix products: 42.6 us -> 20.1 us  [the longest x1 7.86 us: local_step(): q_proj = jnp.dot(normed, w_q, preferred_element_type=F32).astype(BF16)]
    convert_element_type x5 -> x3, other arithmetic: 6.92 us -> 3.01 us  [the longest x1 1.48 us: local_step(): lax.dynamic_slice(x_in, (row0, lax.rem(sp, CORES) * half), (SUBROWS, half))]
  transfers between devices with their start and end apart: 3 -> 0, of which waited for: 3 -> 0; matrix products, arithmetic and copies ran while one was open for 0% -> 0% of each run, Pallas kernels for 0% -> 0%
where the time goes in v1:
time: 140 us
  Pallas kernels  88.9 us (64%)
  other arithmetic  22.8 us (16%)
  matrix products  20.1 us (14%)
  local copies, waits for them, and re-layouts  7.01 us (5%)
    pallas_call x1, Pallas kernels, rest_of_layer(): pl.pallas_call(functools.partial(rest_kernel, nx, ny, dim), out_shape=jax...  88.9 us
    select_n x1, other arithmetic, local_step(): v_out = jnp.where(slot_hit, v_new[:, None], v_cache)  14.1 us
    dot_general x1, matrix products, local_step(): q_proj = jnp.dot(normed, w_q, preferred_element_type=F32).astype(BF16)  7.86 us
    dot_general x1, matrix products, local_step(): jnp.einsum('bkgt,btkd->bkgd', weights.astype(BF16), v_out, preferred_elem...  4.43 us
    dot_general x1, matrix products, local_step(): k_proj = jnp.dot(normed, w_k, preferred_element_type=F32).astype(BF16)  3.1 us
    unnamed x15, local copies, waits for them, and re-layouts  2.89 us

profile of v1, /device:TPU:97, one launch (start us, length us, event | category | flops | bytes accessed | tf_op | source)
XLA Modules:
  0.0 139.7 jit_solution(5391954795499619169)
XLA Ops:
  0.6 0.0 copy-start
  0.7 0.8 convert_element_type.44
  1.5 1.9 %fusion.4 = f32[128]{0:T(128)S(1)} fusion(bf16[128,6144]{1,0:T(8,128)(2,1)} %param.13), kind=kLoop, calls=%fused_computation.8 | loop fusion | flops 2359168 | bytes 1573376 | tf_op jit(solution)/shard_map/reduce_sum | solution.py:24
  3.4 0.7 convert_element_type.41
  4.1 1.3 reshape.180
  5.4 0.7 broadcast_compare_fusion.1
  6.2 0.2 multiply_cosine_fusion
  6.4 0.1 copy.35
  6.5 0.1 copy.36
  6.6 0.0 copy-done
  6.6 2.0 %convolution_convert_fusion.1 = bf16[128,256]{1,0:T(8,128)(2,1)S(1)} fusion(bf16[6144,256]{1,0:T(8,128)(2,1)S(1)} %copy-done, bf16[128,6144]{1,0:T(8,128)(2,1)} %param.13, f32[6144]{0:T(1024)S(1)} %convert_element_type.41, f32[128]{0:T(128)S(1)} %add_rsqrt_fusion), kind=kOutput, calls=%fused_computation.17 | convolution fusion | flops 405831680 | bytes 4809216 | tf_op jit(solution)/shard_map/dot_general | solution.py:393
  8.7 0.0 copy-start.5
  8.7 1.5 %dynamic-slice_convert_fusion.own_x_ref = f32[8,3072]{1,0:T(8,128)} fusion(bf16[128,6144]{1,0:T(8,128)(2,1)} %param.13, s32[]{:T(128)S(6)} %select_n.30, s32[]{:T(128)S(6)} %select_n.31), kind=kLoop, calls=%fused_computation.39 | loop fusion | flops 24576 | bytes 147464 | tf_op jit(solution)/shard_map/convert_element_type | solution.py:414
  10.2 0.0 copy-start.3
  10.2 3.1 %fusion.14 = f32[128,256]{1,0:T(8,128)S(1)} fusion(bf16[6144,256]{1,0:T(8,128)(2,1)} %param.19, bf16[128,6144]{1,0:T(8,128)(2,1)} %param.13, f32[6144]{0:T(1024)S(1)} %convert_element_type.41, f32[128]{0:T(128)S(1)} %add_rsqrt_fusion), kind=kOutput, calls=%fused_computation.19 | convolution fusion | flops 405864448 | bytes 4874752 | tf_op jit(solution)/shard_map/dot_general | solution.py:392
  13.3 0.1 reshape.179
  13.3 0.3 subtract_convert_fusion.1
  13.6 0.2 pad_maximum_fusion
  13.8 0.0 copy-done.3
  13.8 0.0 copy-start.4
  13.8 7.9 %fusion.7 = f32[128,1536]{1,0:T(8,128)S(1)} fusion(bf16[6144,1536]{1,0:T(8,128)(2,1)} %param.18, bf16[128,6144]{1,0:T(8,128)(2,1)S(1)} %copy-done.3, f32[6144]{0:T(1024)S(1)} %convert_element_type.41, f32[128]{0:T(128)S(1)} %add_rsqrt_fusion), kind=kOutput, calls=%fused_computation.12 | convolution fusion | flops 2419458048 | bytes 21258752 | tf_op jit(solution)/shard_map/dot_general | solution.py:391
  21.7 0.3 copy.32
  22.0 0.1 subtract_convert_fusion
  22.1 0.4 copy.34
  22.5 0.4 copy.33
  23.0 0.0 copy-done.5
  23.0 0.0 copy-done.4
  23.0 14.1 %broadcast_select_fusion = (bf16[128,64,2,128]{3,2,1,0:T(2,128)(2,1)}, bf16[128,64,2,128]{3,2,1,0:T(2,128)(2,1)S(1)}) fusion(bf16[128,64,2,128]{3,2,1,0:T(2,128)(2,1)} %param.16, pred[128,64]{1,0:T(8,128)(4,1)S(1)} %get-tuple-element.12, bf16[128,2,128]{2,1,0:T(2,128)(2,1)S(1)} %broadcast_in_dim.65, bf16[128,64,2,128]{3,2,1,0:T(2,128)(2,1)} %param.15, ...), kind=kLoop, calls=%fused_computation | loop fusion | flops 4194304 | bytes 16916480 | tf_op jit(solution)/shard_map/jit(_where)/select_n | solution.py:401
  37.1 0.0 copy-start.2
  37.1 2.7 %fusion.31 = (f32[128,2,6]{2,1,0:T(2,128)S(1)}, f32[128,2,6,64]{3,2,1,0:T(8,128)S(1)}) fusion(bf16[128,64,2,128]{3,2,1,0:T(2,128)(2,1)S(1)} %get-tuple-element.23, bf16[128,2,6,64]{3,2,1,0:T(8,128)(2,1)S(1)} %copy.34, bf16[128,2,6,64]{3,2,1,0:T(8,128)(2,1)S(1)} %copy.33, pred[128,64]{1,0:T(8,128)(4,1)S(1)} %get-tuple-element.11), kind=kOutput, calls=%fused_computation.49 | convolution fusion | flops 26245632 | bytes 4995072 | tf_op jit(solution)/shard_map/bkgd,btkd->bkgt/dot_general | solution.py:403
  39.8 0.0 copy-done.2
  39.8 0.1 copy.43
  39.9 0.8 fusion.17
  40.7 4.4 %fusion = f32[128,2,6,128]{3,2,1,0:T(8,128)} fusion(bf16[128,64,2,128]{3,2,1,0:T(2,128)(2,1)} %get-tuple-element.24, f32[128,2,6,64]{3,2,1,0:T(8,128)S(1)} %get-tuple-element.16, f32[128,2,6]{2,1,0:T(2,128)S(1)} %get-tuple-element.15, pred[128,64]{1,0:T(8,128)(4,1)S(1)} %get-tuple-element.11), kind=kOutput, calls=%fused_computation.2 | convolution fusion | flops 25460736 | bytes 5388288 | tf_op jit(solution)/shard_map/bkgt,btkd->bkgd/dot_general | solution.py:409
  45.2 1.5 %copy.39 = f32[128,2,6,128]{0,3,2,1:T(8,128)S(1)} copy(f32[128,2,6,128]{3,2,1,0:T(8,128)} %fusion) | data formatting | bytes 1572864 | tf_op jit(solution)/shard_map/bkgt,btkd->bkgd/dot_general | solution.py:409
  46.7 0.1 copy.44
  46.8 0.1 fusion.15
  46.8 1.2 copy.42
  48.1 0.0 copy-start.1
  48.1 88.9 %rest_of_layer.1 = bf16[128,6144]{1,0:T(8,128)(2,1)} custom-call(f32[2,4,32,896]{3,2,1,0:T(8,128)} %bitcast.11, f32[8,3072]{1,0:T(8,128)} %dynamic-slice_convert_fusion.own_x_ref, f32[2,1,3072]{2,1,0:T(1,128)} %bitcast.16, bf16[1536,6144]{1,0:T(8,128)(2,1)} %wo_hbm.1, bf16[6144,512]{1,0:T(8,128)(2,1)} %w1_hbm.1, bf16[6144,512]{1,0:T(8,128)(2,1)} %w3_hbm.1, ...), custom_call_target="tpu_custom_call" | custom-call | tf_op jit(solution)/shard_map/rest_of_layer/pallas_call | solution.py:365
  137.0 2.7 %copy.56 = bf16[128,6144]{1,0:T(8,128)(2,1)} copy(bf16[128,6144]{1,0:T(8,128)(2,1)} %rest_of_layer.1) | data formatting | bytes 3145728
  139.7 0.0 copy-done.1
  (4 shorter events, 0.0 us)
Async XLA Ops:
  0.6 6.0 %copy-start = (bf16[6144,256]{1,0:T(8,128)(2,1)S(1)}, bf16[6144,256]{1,0:T(8,128)(2,1)}, u32[]{:S(2)}) copy-start(bf16[6144,256]{1,0:T(8,128)(2,1)} %param.20) | copy-start | bytes 9437188
  8.7 14.3 %copy-start.5 = (bf16[128,2,128]{2,1,0:T(2,128)(2,1)}, bf16[128,2,128]{2,1,0:T(2,128)(2,1)S(1)}, u32[]{:S(2)}) copy-start(bf16[128,2,128]{2,1,0:T(2,128)(2,1)S(1)} %broadcast_in_dim.65) | copy-start | bytes 196612
  10.2 3.7 %copy-start.3 = (bf16[128,6144]{1,0:T(8,128)(2,1)S(1)}, bf16[128,6144]{1,0:T(8,128)(2,1)}, u32[]{:S(2)}) copy-start(bf16[128,6144]{1,0:T(8,128)(2,1)} %param.13) | copy-start | bytes 4718596
  13.8 9.2 %copy-start.4 = (bf16[128,2,128]{2,1,0:T(2,128)(2,1)}, bf16[128,2,128]{2,1,0:T(2,128)(2,1)S(1)}, u32[]{:S(2)}) copy-start(bf16[128,2,128]{2,1,0:T(2,128)(2,1)S(1)} %pad_maximum_fusion) | copy-start | bytes 196612
  37.1 2.7 %copy-start.2 = (bf16[128,64,2,128]{3,2,1,0:T(2,128)(2,1)}, bf16[128,64,2,128]{3,2,1,0:T(2,128)(2,1)S(1)}, u32[]{:S(2)}) copy-start(bf16[128,64,2,128]{3,2,1,0:T(2,128)(2,1)S(1)} %get-tuple-element.23) | copy-start | bytes 12582916
  48.1 91.6 %copy-start.1 = (bf16[6144,256]{1,0:T(8,128)(2,1)S(1)}, bf16[6144,256]{1,0:T(8,128)(2,1)}, u32[]{:S(2)}) copy-start(bf16[6144,256]{1,0:T(8,128)(2,1)} %param.20) | copy-start | bytes 9437188

commit v2 on v1

--- a/solution.py
+++ b/solution.py
@@ -19,25 +19,12 @@
 BF16 = jnp.bfloat16
 
 
-def rms_norm(row_vals, gain_vec):
-    vals32 = row_vals.astype(F32)
-    inv_rms = lax.rsqrt(jnp.mean(vals32 * vals32, axis=-1, keepdims=True) + NORM_EPS)
-    return (vals32 * inv_rms * gain_vec.astype(F32)).astype(BF16)
-
-
 def rotary_tables(positions, head_dim):
     half_dim = head_dim // 2
     inv_freq = ROPE_THETA ** (jnp.arange(half_dim, dtype=F32) * (-2.0 / head_dim))
     angles = positions.astype(F32)[:, None] * inv_freq[None, :]
-    return jnp.cos(angles), jnp.sin(angles)
-
-
-def apply_rotary(head_vecs, cos_part, sin_part):
-    half_dim = head_vecs.shape[-1] // 2
-    cos_part, sin_part = cos_part[:, None, :], sin_part[:, None, :]
-    lower_half = head_vecs[..., :half_dim]
-    upper_half = head_vecs[..., half_dim:]
-    return jnp.concatenate([lower_half * cos_part - upper_half * sin_part, upper_half * cos_part + lower_half * sin_part], axis=-1)
+    cos_part, sin_part = jnp.cos(angles), jnp.sin(angles)
+    return jnp.concatenate([cos_part, cos_part], axis=-1), jnp.concatenate([-sin_part, sin_part], axis=-1)
 
 
 def run_together(*flows):
@@ -65,9 +52,9 @@
 
 def rest_kernel(
     nx, ny, dim,
-    part_ref, own_x_ref, gain_ref, wo_hbm, w1_hbm, w3_hbm, w2_hbm,
+    part_ref, gain_ref, x_hbm, wo_hbm, w1_hbm, w3_hbm, w2_hbm,
     out_ref,
-    wo_v, w1_v, w3_v, w2_v, load_sem,
+    own_x, wo_v, w1_v, w3_v, w2_v, load_sem,
     pair_in, ring_a, ring_a_in, o_in, proj, proj_in, stat_out, stat_in,
     gathered, normed, other, other_in, mine, big_in, small_in, final,
     send_sem, recv_sem,
@@ -96,6 +83,7 @@
         return copy
 
     my_cols = pl.ds(pl.multiple_of(core * half, half), half)
+    x_load = load(x_hbm.at[ix * ny + iy, :, my_cols], own_x)
     wo_load = load(wo_hbm.at[:, my_cols], wo_v)
     w1_load = load(w1_hbm, w1_v)
     w3_load = load(w3_hbm, w3_v)
@@ -208,7 +196,8 @@
         return proj.at[t, :, pl.ds(h * (half // 2), half // 2)]
 
     run_together(ring_reduce(proj_piece, proj_in, on_y, y_right, y_left, add_into, lambda: None))
-    x_mid = (own_x_ref[...] + proj[iy]).astype(BF16).astype(F32)
+    x_load.wait()
+    x_mid = (own_x[...].astype(F32) + proj[iy]).astype(BF16).astype(F32)
 
     square = jnp.sum(x_mid * x_mid, axis=-1, keepdims=True)
     stat_out[...] = jnp.broadcast_to(square, stat_out.shape)
@@ -323,6 +312,177 @@
         out_ref[:, c * half : (c + 1) * half] = final[c].reshape(rows, half).astype(BF16)
     for copy in sent:
         copy.wait_send()
+
+
+def front_kernel(
+    group_size, kv_local,
+    x_ref, gain_ref, cos_ref, sin_ref, pos_ref, wq_hbm, wk_hbm, wv_hbm, k_hbm, v_hbm,
+    parts_ref, k_out_hbm, v_out_hbm, k_new_ref, v_new_ref,
+    wq_v, wk_v, wv_v, k_buf, v_buf, normed, q_rows, num_rows, max_rows, sum_rows, k_rows, v_rows,
+    load_sem, store_sem,
+):
+    rows, dim = x_ref.shape
+    columns = k_buf.shape[1]
+    block_len = columns // kv_local
+    head_dim = k_buf.shape[2]
+    slots = SUBROWS * kv_local
+    first_slot = lax.axis_index("sp") * block_len
+    scale = head_dim ** -0.5
+
+    loads = []
+
+    def load(src, dst):
+        copy = pltpu.make_async_copy(src, dst, load_sem.at[len(loads)])
+        copy.start()
+        loads.append(copy)
+        return copy
+
+    step = 2 * head_dim
+    q_steps = wq_v.shape[1] // step
+    early = q_steps // 2
+    wk_load = load(wk_hbm, wk_v)
+    wv_load = load(wv_hbm, wv_v)
+    q_loads = [load(wq_hbm.at[:, pl.ds(j * step, step)], wq_v.at[:, pl.ds(j * step, step)]) for j in range(early)]
+    k_load = load(k_hbm, k_buf)
+    v_load = load(v_hbm, v_buf)
+    q_loads += [load(wq_hbm.at[:, pl.ds(j * step, step)], wq_v.at[:, pl.ds(j * step, step)]) for j in range(early, q_steps)]
+
+    q_rows[...] = jnp.zeros_like(q_rows)
+    block = 2 * SUBROWS
+
+    @pl.loop(0, rows // block)
+    def _(i):
+        at = pl.ds(pl.multiple_of(i * block, block), block)
+        vals = x_ref[at, :].astype(F32)
+        inv_rms = lax.rsqrt(jnp.mean(vals * vals, axis=-1, keepdims=True) + NORM_EPS)
+        normed[at, :] = (vals * inv_rms * gain_ref[...]).astype(BF16)
+
+    def rotate(vals):
+        vals = vals.astype(BF16).astype(F32)
+        return (vals * cos_ref[...] + pltpu.roll(vals, head_dim // 2, 1) * sin_ref[...]).astype(BF16)
+
+    wk_load.wait()
+    k_proj = jnp.dot(normed[...], wk_v[...], preferred_element_type=F32)
+    for k in range(kv_local):
+        cols = slice(k * head_dim, (k + 1) * head_dim)
+        rotated = rotate(k_proj[:, cols])
+        k_new_ref[:, cols] = rotated
+        k_rows[pl.ds(k, rows, stride=kv_local), :] = rotated.astype(F32)
+    wv_load.wait()
+    v_proj = jnp.dot(normed[...], wv_v[...], preferred_element_type=F32).astype(BF16)
+    v_new_ref[...] = v_proj
+    for k in range(kv_local):
+        v_rows[pl.ds(k, rows, stride=kv_local), :] = v_proj[:, k * head_dim : (k + 1) * head_dim].astype(F32)
+
+    def project(j):
+        q_loads[j].wait()
+        prod = jnp.dot(normed[...], wq_v[:, j * step : (j + 1) * step], preferred_element_type=F32)
+        for n in range(step // head_dim):
+            head = j * (step // head_dim) + n
+            row = head // group_size * SUBROWS + head % group_size
+            q_rows[pl.ds(row, rows, stride=slots), :] = rotate(prod[:, n * head_dim : (n + 1) * head_dim]).astype(F32)
+
+    for j in range(early + 1):
+        project(j)
+    k_load.wait()
+    v_load.wait()
+    sub = lax.broadcasted_iota(jnp.int32, (block, head_dim), 0)
+    per_block = block // kv_local
+
+    @pl.loop(0, rows)
+    def _(b):
+        p = pos_ref[b] - first_slot
+
+        @pl.when((p >= 0) & (p < block_len))
+        def _():
+            at = pl.ds(pl.multiple_of(p // per_block * block, block), block)
+            hit = sub // kv_local == p % per_block
+            for buf, new_rows in ((k_buf, k_rows), (v_buf, v_rows)):
+                new = new_rows[pl.ds(b * kv_local, 1), :]
+                for k in range(1, kv_local):
+                    new = jnp.where(sub % kv_local == k, new_rows[pl.ds(b * kv_local + k, 1), :], new)
+                buf[b, at, :] = jnp.where(hit, new, buf[b, at, :].astype(F32)).astype(BF16)
+
+    for j in range(early + 1, q_steps):
+        project(j)
+    stores = [
+        pltpu.make_async_copy(k_buf, k_out_hbm, store_sem.at[0]),
+        pltpu.make_async_copy(v_buf, v_out_hbm, store_sem.at[1]),
+    ]
+    for store in stores:
+        store.start()
+
+    col = lax.broadcasted_iota(jnp.int32, (slots, columns), 1)
+    own_head = col % kv_local == lax.broadcasted_iota(jnp.int32, (slots, columns), 0) // SUBROWS
+    time = jnp.where(own_head, first_slot + col // kv_local, jnp.iinfo(jnp.int32).max)
+    together = SUBROWS
+
+    @pl.loop(0, rows // together)
+    def _(i):
+        for u in range(together):
+            b = i * together + u
+            at = pl.ds(pl.multiple_of(b * slots, slots), slots)
+            scores = lax.dot_general(q_rows[at, :].astype(BF16), k_buf[b], (((1,), (1,)), ((), ())), preferred_element_type=F32) * scale
+            valid = time <= pos_ref[b]
+            scores = jnp.where(valid, scores, MASK_FILL)
+            top = jnp.max(scores, axis=-1, keepdims=True)
+            weights = jnp.where(valid, jnp.exp(scores - top), 0.0)
+            total = jnp.sum(weights, axis=-1, keepdims=True)
+            num_rows[at, :] = jnp.dot(weights.astype(BF16), v_buf[b], preferred_element_type=F32)
+            max_rows[at, :] = jnp.broadcast_to(top, (slots, LANES))
+            sum_rows[at, :] = jnp.broadcast_to(total, (slots, LANES))
+
+    lane = lax.broadcasted_iota(jnp.int32, (rows, LANES), 1)
+    width = group_size * head_dim
+    for k in range(kv_local):
+        stats = jnp.zeros((rows, LANES), F32)
+        for g in range(group_size):
+            at = pl.ds(k * SUBROWS + g, rows, stride=slots)
+            parts_ref[k, :, g * head_dim : (g + 1) * head_dim] = num_rows[at, :]
+            stats = jnp.where(lane == g, max_rows[at, :], stats)
+            stats = jnp.where(lane == LANES // 2 + g, sum_rows[at, :], stats)
+        parts_ref[k, :, width:] = stats
+    for store in stores:
+        store.wait()
+
+
+def front_of_layer(x_in, gain, cos_part, sin_part, positions, w_q, w_k, w_v, k_flat, v_flat, kv_local):
+    rows, dim = x_in.shape
+    columns, head_dim = k_flat.shape[1:]
+    group_size = w_q.shape[1] // head_dim // kv_local
+    assert group_size <= SUBROWS
+    slots = SUBROWS * kv_local
+    hbm_spec = pl.BlockSpec(memory_space=pltpu.HBM)
+    vmem_spec = pl.BlockSpec(memory_space=pltpu.VMEM)
+    smem_spec = pl.BlockSpec(memory_space=pltpu.SMEM)
+    kv_width = w_k.shape[1]
+    row_buf = pltpu.VMEM((rows * slots, LANES), F32)
+    new_buf = pltpu.VMEM((rows * kv_local, head_dim), F32)
+    return pl.pallas_call(
+        functools.partial(front_kernel, group_size, kv_local),
+        out_shape=(
+            jax.ShapeDtypeStruct((kv_local, rows, group_size * head_dim + LANES), F32),
+            jax.ShapeDtypeStruct(k_flat.shape, BF16),
+            jax.ShapeDtypeStruct(v_flat.shape, BF16),
+            jax.ShapeDtypeStruct((rows, kv_width), BF16),
+            jax.ShapeDtypeStruct((rows, kv_width), BF16),
+        ),
+        in_specs=[vmem_spec] * 4 + [smem_spec] + [hbm_spec] * 5,
+        out_specs=(vmem_spec, hbm_spec, hbm_spec, vmem_spec, vmem_spec),
+        scratch_shapes=[
+            pltpu.VMEM(w_q.shape, BF16),
+            pltpu.VMEM(w_k.shape, BF16),
+            pltpu.VMEM(w_v.shape, BF16),
+            pltpu.VMEM(k_flat.shape, BF16),
+            pltpu.VMEM(v_flat.shape, BF16),
+            pltpu.VMEM(x_in.shape, BF16),
+            row_buf, row_buf, row_buf, row_buf, new_buf, new_buf,
+            pltpu.SemaphoreType.DMA((w_q.shape[1] // (2 * head_dim) + 4,)),
+            pltpu.SemaphoreType.DMA((2,)),
+        ],
+        compiler_params=pltpu.CompilerParams(vmem_limit_bytes=56 * 1024 * 1024),
+        name="front_of_layer",
+    )(x_in, gain, cos_part, sin_part, positions, w_q, w_k, w_v, k_flat, v_flat)
 
 
 def rest_of_layer(mesh, parts, own_x, gain, w_o, w_gate, w_up, w_down):
@@ -338,11 +498,12 @@
     chunk_rows = ny * SUBROWS
     count = 152
     scratch = [
+        pltpu.VMEM((SUBROWS, half), BF16),
         pltpu.VMEM((w_o.shape[0], half), BF16),
         pltpu.VMEM(w_gate.shape, BF16),
         pltpu.VMEM(w_up.shape, BF16),
         pltpu.VMEM(w_down.shape, BF16),
-        pltpu.SemaphoreType.DMA((4,)),
+        pltpu.SemaphoreType.DMA((5,)),
         pltpu.VMEM((nx, chunk_rows, width), F32),
         pltpu.VMEM((nx, chunk_rows, width), F32),
         pltpu.VMEM((6, chunk_rows // 2, width), F32),
@@ -365,12 +526,12 @@
     return pl.pallas_call(
         functools.partial(rest_kernel, nx, ny, dim),
         out_shape=jax.ShapeDtypeStruct((rows, dim), BF16),
-        in_specs=[vmem_spec] * 3 + [any_spec] * 4,
+        in_specs=[vmem_spec] * 2 + [any_spec] * 5,
         out_specs=vmem_spec,
         scratch_shapes=scratch,
         compiler_params=pltpu.CompilerParams(collective_id=0, has_side_effects=True, vmem_limit_bytes=60 * 1024 * 1024),
         name="rest_of_layer",
-    )(parts, own_x, gain, w_o, w_gate, w_up, w_down)
+    )(parts, gain, own_x, w_o, w_gate, w_up, w_down)
 
 
 def solution(mesh):
@@ -385,33 +546,16 @@
         num_rows, block_len, kv_local, head_dim = k_cache.shape
         dim = x_in.shape[1]
         half = dim // CORES
-        heads_local = w_q.shape[1] // head_dim
-        group_size = heads_local // kv_local
-        normed = rms_norm(x_in, attn_gain)
-        q_proj = jnp.dot(normed, w_q, preferred_element_type=F32).astype(BF16)
-        k_proj = jnp.dot(normed, w_k, preferred_element_type=F32).astype(BF16)
-        v_new = jnp.dot(normed, w_v, preferred_element_type=F32).astype(BF16).reshape(num_rows, kv_local, head_dim)
         cos_part, sin_part = rotary_tables(positions, head_dim)
-        q_rot = apply_rotary(q_proj.astype(F32).reshape(num_rows, heads_local, head_dim), cos_part, sin_part).astype(BF16)
-        k_new = apply_rotary(k_proj.astype(F32).reshape(num_rows, kv_local, head_dim), cos_part, sin_part).astype(BF16)
-        sp = lax.axis_index('sp')
-        slot_ids = sp * block_len + jnp.arange(block_len)
-        slot_hit = (slot_ids[None, :] == positions[:, None])[:, :, None, None]
-        k_out = jnp.where(slot_hit, k_new[:, None], k_cache)
-        v_out = jnp.where(slot_hit, v_new[:, None], v_cache)
-        q_grouped = q_rot.reshape(num_rows, kv_local, group_size, head_dim)
-        scores = jnp.einsum('bkgd,btkd->bkgt', q_grouped, k_out, preferred_element_type=F32) * (head_dim ** -0.5)
-        is_valid = (slot_ids[None, :] <= positions[:, None])[:, None, None, :]
-        scores = jnp.where(is_valid, scores, MASK_FILL)
-        local_max = jnp.max(scores, axis=-1)
-        weights = jnp.where(is_valid, jnp.exp(scores - local_max[..., None]), 0.0)
-        local_sum = jnp.sum(weights, axis=-1)
-        local_num = jnp.einsum('bkgt,btkd->bkgd', weights.astype(BF16), v_out, preferred_element_type=F32)
-        gap = ((0, 0), (0, 0), (0, LANES // 2 - group_size))
-        parts = jnp.concatenate([local_num.reshape(num_rows, kv_local, group_size * head_dim), jnp.pad(local_max, gap), jnp.pad(local_sum, gap)], axis=-1)
-        parts = parts.transpose(1, 0, 2).reshape(kv_local, nx, num_rows // nx, -1)
-        row0 = ((sp // CORES) * ny + lax.axis_index('tp')) * SUBROWS
-        own_x = lax.dynamic_slice(x_in, (row0, lax.rem(sp, CORES) * half), (SUBROWS, half)).astype(F32)
+        flat = (num_rows, block_len * kv_local, head_dim)
+        parts, k_out, v_out, k_new, v_new = front_of_layer(
+            x_in, attn_gain.astype(F32)[None, :], cos_part, sin_part, positions, w_q, w_k, w_v,
+            k_cache.reshape(flat), v_cache.reshape(flat), kv_local,
+        )
+        k_out, v_out = k_out.reshape(k_cache.shape), v_out.reshape(v_cache.shape)
+        k_new, v_new = k_new.reshape(num_rows, kv_local, head_dim), v_new.reshape(num_rows, kv_local, head_dim)
+        parts = parts.reshape(kv_local, nx, num_rows // nx, parts.shape[-1])
+        own_x = x_in.reshape(nx * ny, SUBROWS, dim)
         gain = mlp_gain.astype(F32).reshape(CORES, 1, half)
         x_out = rest_of_layer(mesh, parts, own_x, gain, w_o, w_gate, w_up, w_down)
         return x_out, k_out, v_out, k_new, v_new

time: 140 us -> 149 us (1.064)
  Pallas kernels: 88.9 us -> 138 us
  matrix products: 20.1 us -> 0 us
  other arithmetic: 22.8 us -> 4.36 us
    pallas_call x0 -> x1, Pallas kernels: none -> 48.9 us  [front_of_layer(): pl.pallas_call(functools.partial(front_kernel, group_size, kv_local), out...]
    dot_general x5 -> x0, matrix products: 20.1 us -> none  [the longest x1 7.86 us: local_step(): q_proj = jnp.dot(normed, w_q, preferred_element_type=F32).astype(BF16)]
    select_n x1 -> x0, other arithmetic: 14.1 us -> none  [local_step(): v_out = jnp.where(slot_hit, v_new[:, None], v_cache)]
    reduce_sum x2 -> x0, other arithmetic: 2.73 us -> none  [the longest x1 1.9 us: rms_norm(): jnp.mean(vals32 * vals32, axis=-1, keepdims=True) + NORM_EPS]
    reshape x2, local copies, waits for them, and re-layouts: 0.33 us -> 2.98 us  [the longest x1 1.49 us: local_step(): k_new.reshape(num_rows, kv_local, head_dim)]
    convert_element_type x2 -> x0, other arithmetic: 2.2 us -> none  [the longest x1 1.48 us: local_step(): lax.dynamic_slice(x_in, (row0, lax.rem(sp, CORES) * half), (SUBROWS, half))]
    dot_general x1 -> x0, local copies, waits for them, and re-layouts: 1.51 us -> none  [local_step(): jnp.einsum('bkgt,btkd->bkgd', weights.astype(BF16), v_out, preferred_elem...]
where the time goes in v2:
time: 149 us; the launch traced here: 148 us
  Pallas kernels  138 us (93%)
  local copies, waits for them, and re-layouts  5.67 us (4%)
  other arithmetic  4.36 us (3%)
    pallas_call x1, Pallas kernels, rest_of_layer(): pl.pallas_call(functools.partial(rest_kernel, nx, ny, dim), out_shape=jax...  88.8 us
    pallas_call x1, Pallas kernels, front_of_layer(): pl.pallas_call(functools.partial(front_kernel, group_size, kv_local), out...  48.9 us

profile of v2, /device:TPU:97, one launch (start us, length us, event | category | flops | bytes accessed | tf_op | source)
XLA Modules:
  0.0 148.4 jit_solution(3101831278871653853)
XLA Ops:
  0.6 0.7 convert_element_type.2
  1.3 1.3 broadcast_in_dim.9
  2.6 1.3 reshape.56
  3.9 0.3 fusion
  4.2 0.8 pad_maximum_fusion
  5.0 48.9 %front_of_layer.1 = (f32[2,128,896]{2,1,0:T(8,128)}, bf16[128,128,128]{2,1,0:T(8,128)(2,1)}, bf16[128,128,128]{2,1,0:T(8,128)(2,1)}, bf16[128,256]{1,0:T(8,128)(2,1)}, bf16[128,256]{1,0:T(8,128)(2,1)}) custom-call(bf16[128,6144]{1,0:T(8,128)(2,1)} %x_ref.1, f32[1,6144]{1,0:T(1,128)} %bitcast.12, f32[128,128]{1,0:T(8,128)} %get-tuple-element.18.cos_ref, ...), custom_call_target="tpu_custom_call" | custom-call | tf_op jit(solution)/shard_map/front_of_layer/pallas_call | solution.py:461
  53.9 1.5 %reshape.53 = bf16[128,2,128]{2,1,0:T(2,128)(2,1)} reshape(bf16[128,256]{1,0:T(8,128)(2,1)} %get-tuple-element.13) | data formatting | bytes 131072 | tf_op jit(solution)/shard_map/reshape | solution.py:556
  55.4 1.5 %reshape.54 = bf16[128,2,128]{2,1,0:T(2,128)(2,1)} reshape(bf16[128,256]{1,0:T(8,128)(2,1)} %get-tuple-element.14) | data formatting | bytes 131072 | tf_op jit(solution)/shard_map/reshape | solution.py:556
  56.9 88.8 %rest_of_layer.1 = bf16[128,6144]{1,0:T(8,128)(2,1)} custom-call(f32[2,4,32,896]{3,2,1,0:T(8,128)} %bitcast.11, f32[2,1,3072]{2,1,0:T(1,128)} %bitcast.13, bf16[16,8,6144]{2,1,0:T(8,128)(2,1)} %bitcast.8, bf16[1536,6144]{1,0:T(8,128)(2,1)} %wo_hbm.1, bf16[6144,512]{1,0:T(8,128)(2,1)} %w1_hbm.1, bf16[6144,512]{1,0:T(8,128)(2,1)} %w3_hbm.1, ...), custom_call_target="tpu_custom_call" | custom-call | tf_op jit(solution)/shard_map/rest_of_layer/pallas_call | solution.py:526
  145.7 2.7 %copy.19 = bf16[128,6144]{1,0:T(8,128)(2,1)} copy(bf16[128,6144]{1,0:T(8,128)(2,1)} %rest_of_layer.1) | data formatting | bytes 3145728
  (1 shorter events, 0.0 us)

commit v3 on v2

--- a/solution.py
+++ b/solution.py
@@ -52,9 +52,9 @@
 
 def rest_kernel(
     nx, ny, dim,
-    part_ref, gain_ref, x_hbm, wo_hbm, w1_hbm, w3_hbm, w2_hbm,
+    part_ref, gain_ref, x_ref, wo_hbm, w1_hbm, w3_hbm, w2_hbm,
     out_ref,
-    own_x, wo_v, w1_v, w3_v, w2_v, load_sem,
+    wo_v, w1_v, w3_v, w2_v, load_sem,
     pair_in, ring_a, ring_a_in, o_in, proj, proj_in, stat_out, stat_in,
     gathered, normed, other, other_in, mine, big_in, small_in, final,
     send_sem, recv_sem,
@@ -83,7 +83,6 @@
         return copy
 
     my_cols = pl.ds(pl.multiple_of(core * half, half), half)
-    x_load = load(x_hbm.at[ix * ny + iy, :, my_cols], own_x)
     wo_load = load(wo_hbm.at[:, my_cols], wo_v)
     w1_load = load(w1_hbm, w1_v)
     w3_load = load(w3_hbm, w3_v)
@@ -106,55 +105,35 @@
         sent.append(copy)
         return copy
 
-    def ring_reduce(piece, held, at, right, left, add, done):
-        near_r, near_l, far = at(1), at(-1), at(2)
-        r1 = send(piece(far, 0), held.at[0], right)
-        l1 = send(piece(far, 1), held.at[1], left)
-        r2 = send(piece(near_r, 1), held.at[2], right)
-        l2 = send(piece(near_l, 0), held.at[3], left)
-        yield
+    on_ring_x, on_ring_y = (on_x, x_right, x_left), (on_y, y_right, y_left)
+
+    def reduce_begin(piece, held, ring, add):
+        at, right, left = ring
+        r1 = send(piece(at(2), 0), held.at[0], right)
+        l1 = send(piece(at(2), 1), held.at[1], left)
+        r2 = send(piece(at(1), 1), held.at[2], right)
+        l2 = send(piece(at(-1), 0), held.at[3], left)
+        return [piece, held, ring, add, r1, l1, r2, l2]
+
+    def reduce_turn(state):
+        piece, held, (at, right, left), add, r1, l1 = state[:6]
         r1.wait_recv()
-        add(piece(near_r, 0), held.at[0])
-        r3 = send(piece(near_r, 0), held.at[4], right)
+        add(piece(at(1), 0), held.at[0])
+        state.append(send(piece(at(1), 0), held.at[4], right))
         l1.wait_recv()
-        add(piece(near_l, 1), held.at[1])
-        l3 = send(piece(near_l, 1), held.at[5], left)
-        yield
-        me = at(0)
-        l2.wait_recv()
-        add(piece(me, 0), held.at[3])
-        r2.wait_recv()
-        add(piece(me, 1), held.at[2])
-        yield
-        r3.wait_recv()
-        add(piece(me, 0), held.at[4])
-        l3.wait_recv()
-        add(piece(me, 1), held.at[5])
-        done()
-
-    def ring_gather(piece, at, right, left, arrived):
-        me, from_l, from_r, far = at(0), at(-1), at(1), at(2)
-        r1 = send(piece(me, 0), piece(me, 0), right)
-        l1 = send(piece(me, 1), piece(me, 1), left)
-        r2 = send(piece(me, 1), piece(me, 1), right)
-        l2 = send(piece(me, 0), piece(me, 0), left)
-        yield
-        r1.wait_recv()
-        r3 = send(piece(from_l, 0), piece(from_l, 0), right)
-        arrived(piece(from_l, 0))
-        l1.wait_recv()
-        l3 = send(piece(from_r, 1), piece(from_r, 1), left)
-        arrived(piece(from_r, 1))
-        yield
-        r2.wait_recv()
-        arrived(piece(from_l, 1))
-        l2.wait_recv()
-        arrived(piece(from_r, 0))
-        yield
-        r3.wait_recv()
-        arrived(piece(far, 0))
-        l3.wait_recv()
-        arrived(piece(far, 1))
+        add(piece(at(-1), 1), held.at[1])
+        state.append(send(piece(at(-1), 1), held.at[5], left))
+
+    def reduce_end(state):
+        piece, held, (at, _, _), add, _, _, r2, l2, r3, l3 = state
+        for copy, h, k in ((l2, 0, 3), (r2, 1, 2), (r3, 0, 4), (l3, 1, 5)):
+            copy.wait_recv()
+            add(piece(at(0), h), held.at[k])
+
+    def reduce_all(piece, held, ring, add):
+        state = reduce_begin(piece, held, ring, add)
+        reduce_turn(state)
+        reduce_end(state)
 
     def add_into(dst, src):
         dst[...] = dst[...] + src[...]
@@ -173,7 +152,7 @@
     def merge_into(dst, src):
         dst[...] = merge_partials(dst[...], src[...])
 
-    run_together(ring_reduce(part_piece, ring_a_in, on_x, x_right, x_left, merge_into, lambda: None))
+    reduce_all(part_piece, ring_a_in, on_ring_x, merge_into)
     merged = ring_a[on_x(0)]
     stats = merged[:, heads_width:]
     heads = []
@@ -195,57 +174,89 @@
     def proj_piece(t, h):
         return proj.at[t, :, pl.ds(h * (half // 2), half // 2)]
 
-    run_together(ring_reduce(proj_piece, proj_in, on_y, y_right, y_left, add_into, lambda: None))
-    x_load.wait()
-    x_mid = (own_x[...].astype(F32) + proj[iy]).astype(BF16).astype(F32)
+    reduce_all(proj_piece, proj_in, on_ring_y, add_into)
+    x_mid = (x_ref[ix * ny + iy, :, my_cols].astype(F32) + proj[iy]).astype(BF16).astype(F32)
 
     square = jnp.sum(x_mid * x_mid, axis=-1, keepdims=True)
     stat_out[...] = jnp.broadcast_to(square, stat_out.shape)
     swap = send(stat_out, stat_in, partner)
     swap.wait_recv()
     inv_rms = lax.rsqrt((stat_out[:, :1] + stat_in[:, :1]) / dim + NORM_EPS)
-    gathered[core, ix, iy] = (x_mid * inv_rms * gain_ref[core]).astype(BF16).astype(F32)
+    gathered[core, ix, iy] = (x_mid * inv_rms * gain_ref[1:2, my_cols]).astype(BF16).astype(F32)
+
+    quarter, eighth = half // 2, half // 4
+
+    def portion(buf, lo, x_first):
+        def cell(first, second, h=None):
+            cols = pl.ds(lo, quarter) if h is None else pl.ds(lo + h * eighth, eighth)
+            at = (first, second) if x_first else (second, first)
+            return buf.at[(*at, slice(None), cols)]
+
+        return cell, (on_ring_x, on_ring_y) if x_first else (on_ring_y, on_ring_x)
 
     def gather_all(buf):
-        quarter, eighth = half // 2, half // 4
         forwards = []
 
-        def forward(ref_of):
-            ref = ref_of(core)
+        def forward(ref):
             forwards.append(send(ref, ref, partner))
 
-        def at(*index):
-            return lambda c: buf.at[(c, *index)]
-
-        forward(at(ix, iy))
-
-        def flow(lo, y_first):
-            def cols(h):
-                return pl.ds(lo + h * eighth, eighth)
-
-            def along_y_one(t, h):
-                return buf.at[core, ix, t, :, cols(h)]
-
-            def along_x_one(t, h):
-                return buf.at[core, t, iy, :, cols(h)]
-
-            def along_x_all(t, h):
-                return buf.at[core, t, :, :, cols(h)]
-
-            def along_y_all(t, h):
-                return buf.at[core, :, t, :, cols(h)]
-
-            def arrived(ref):
-                forwards.append(send(ref, ref, partner))
-
-            if y_first:
-                yield from ring_gather(along_y_one, on_y, y_right, y_left, arrived)
-                yield from ring_gather(along_x_all, on_x, x_right, x_left, arrived)
-            else:
-                yield from ring_gather(along_x_one, on_x, x_right, x_left, arrived)
-                yield from ring_gather(along_y_all, on_y, y_right, y_left, arrived)
-
-        run_together(flow(0, True), flow(quarter, False))
+        forward(buf.at[core, ix, iy])
+
+        def flow(lo, x_first):
+            cell, (first, second) = portion(buf.at[core], lo, x_first)
+            (f_at, f_right, f_left), (s_at, s_right, s_left) = first, second
+            me = s_at(0)
+
+            def both_ways(ref, right, left):
+                return send(ref, ref, right), send(ref, ref, left)
+
+            def pass_on(copies, from_l, from_r, right, left):
+                copies[0].wait_recv()
+                r = send(from_l(0), from_l(0), right)
+                copies[1].wait_recv()
+                return r, send(from_r(1), from_r(1), left)
+
+            def second_start(t):
+                return both_ways(cell(t, me), s_right, s_left)
+
+            def second_turn(t, copies):
+                far = pass_on(copies, lambda h: cell(t, s_at(-1), h), lambda h: cell(t, s_at(1), h), s_right, s_left)
+                forward(cell(t, s_at(-1)))
+                forward(cell(t, s_at(1)))
+                return far
+
+            def second_end(t, copies):
+                for copy in copies:
+                    copy.wait_recv()
+                forward(cell(t, s_at(2)))
+
+            near = both_ways(cell(f_at(0), me), f_right, f_left)
+            own = second_start(f_at(0))
+            yield
+            far = pass_on(near, lambda h: cell(f_at(-1), me, h), lambda h: cell(f_at(1), me, h), f_right, f_left)
+            from_l, from_r = second_start(f_at(-1)), second_start(f_at(1))
+            forward(cell(f_at(-1), me))
+            forward(cell(f_at(1), me))
+            yield
+            own = second_turn(f_at(0), own)
+            yield
+            for copy in far:
+                copy.wait_recv()
+            from_far = second_start(f_at(2))
+            forward(cell(f_at(2), me))
+            yield
+            from_l, from_r = second_turn(f_at(-1), from_l), second_turn(f_at(1), from_r)
+            yield
+            second_end(f_at(0), own)
+            yield
+            from_far = second_turn(f_at(2), from_far)
+            yield
+            second_end(f_at(-1), from_l)
+            second_end(f_at(1), from_r)
+            yield
+            second_end(f_at(2), from_far)
+
+        run_together(flow(0, False), flow(quarter, True))
         for copy in forwards:
             copy.wait_recv()
 
@@ -277,33 +288,48 @@
         other[:, :, :, cols] = down(1 - core, j)
         swaps.append(send(other.at[:, :, :, cols], other_in.at[:, :, :, cols], partner))
 
-    quarter, eighth = half // 2, half // 4
-
     def reduce_flow(index):
-        lo = index * quarter
-
-        def along_x_all(t, h):
-            return mine.at[t, :, :, pl.ds(lo + h * eighth, eighth)]
-
-        def along_y_all(t, h):
-            return mine.at[:, t, :, pl.ds(lo + h * eighth, eighth)]
-
-        def along_y_one(t, h):
-            return mine.at[ix, t, :, pl.ds(lo + h * eighth, eighth)]
-
-        def along_x_one(t, h):
-            return mine.at[t, iy, :, pl.ds(lo + h * eighth, eighth)]
-
         for j in range(index * tiles // 2, (index + 1) * tiles // 2):
             cols = slice(j * TILE, (j + 1) * TILE)
             swaps[j].wait_recv()
             mine[:, :, :, cols] = down(core, j) + other_in[:, :, :, cols]
-        if index == 0:
-            yield from ring_reduce(along_x_all, big_in.at[0], on_x, x_right, x_left, add_into, lambda: None)
-            yield from ring_reduce(along_y_one, small_in.at[0], on_y, y_right, y_left, add_into, lambda: None)
-        else:
-            yield from ring_reduce(along_y_all, big_in.at[1], on_y, y_right, y_left, add_into, lambda: None)
-            yield from ring_reduce(along_x_one, small_in.at[1], on_x, x_right, x_left, add_into, lambda: None)
+        cell, (first, second) = portion(mine, index * quarter, index == 0)
+        here, there = first[0](0), second[0]
+
+        def begin(k, t):
+            return reduce_begin(lambda to, h: cell(to, t, h), big_in.at[index, k], first, add_into)
+
+        order = (there(2), there(1), there(-1), there(0))
+        states = [begin(k, order[k]) for k in range(2)]
+        yield
+        reduce_turn(states[0])
+        states.append(begin(2, order[2]))
+        yield
+        reduce_turn(states[1])
+        states.append(begin(3, order[3]))
+        yield
+        reduce_turn(states[2])
+        reduce_end(states[0])
+        held = small_in.at[index]
+        _, right, left = second
+
+        def piece(t, h):
+            return cell(here, t, h)
+
+        r1 = send(piece(there(2), 0), held.at[0], right)
+        l1 = send(piece(there(2), 1), held.at[1], left)
+        yield
+        reduce_turn(states[3])
+        reduce_end(states[1])
+        r2 = send(piece(there(1), 1), held.at[2], right)
+        reduce_end(states[2])
+        l2 = send(piece(there(-1), 0), held.at[3], left)
+        yield
+        last = [piece, held, second, add_into, r1, l1, r2, l2]
+        reduce_turn(last)
+        yield
+        reduce_end(states[3])
+        reduce_end(last)
 
     run_together(reduce_flow(0), reduce_flow(1))
     final[core, ix, iy] = (x_mid + mine[ix, iy]).astype(BF16).astype(F32)
@@ -355,7 +381,7 @@
         at = pl.ds(pl.multiple_of(i * block, block), block)
         vals = x_ref[at, :].astype(F32)
         inv_rms = lax.rsqrt(jnp.mean(vals * vals, axis=-1, keepdims=True) + NORM_EPS)
-        normed[at, :] = (vals * inv_rms * gain_ref[...]).astype(BF16)
+        normed[at, :] = (vals * inv_rms * gain_ref[:1, :]).astype(BF16)
 
     def rotate(vals):
         vals = vals.astype(BF16).astype(F32)
@@ -365,14 +391,13 @@
     k_proj = jnp.dot(normed[...], wk_v[...], preferred_element_type=F32)
     for k in range(kv_local):
         cols = slice(k * head_dim, (k + 1) * head_dim)
-        rotated = rotate(k_proj[:, cols])
-        k_new_ref[:, cols] = rotated
-        k_rows[pl.ds(k, rows, stride=kv_local), :] = rotated.astype(F32)
+        k_rows[pl.ds(k, rows, stride=kv_local), :] = rotate(k_proj[:, cols]).astype(F32)
+    k_new_ref[...] = k_rows[...].astype(BF16)
     wv_load.wait()
     v_proj = jnp.dot(normed[...], wv_v[...], preferred_element_type=F32).astype(BF16)
-    v_new_ref[...] = v_proj
     for k in range(kv_local):
         v_rows[pl.ds(k, rows, stride=kv_local), :] = v_proj[:, k * head_dim : (k + 1) * head_dim].astype(F32)
+    v_new_ref[...] = v_rows[...].astype(BF16)
 
     def project(j):
         q_loads[j].wait()
@@ -415,22 +440,29 @@
     col = lax.broadcasted_iota(jnp.int32, (slots, columns), 1)
     own_head = col % kv_local == lax.broadcasted_iota(jnp.int32, (slots, columns), 0) // SUBROWS
     time = jnp.where(own_head, first_slot + col // kv_local, jnp.iinfo(jnp.int32).max)
-    together = SUBROWS
+    together = 16
 
     @pl.loop(0, rows // together)
     def _(i):
-        for u in range(together):
-            b = i * together + u
-            at = pl.ds(pl.multiple_of(b * slots, slots), slots)
-            scores = lax.dot_general(q_rows[at, :].astype(BF16), k_buf[b], (((1,), (1,)), ((), ())), preferred_element_type=F32) * scale
+        group = [i * together + u for u in range(together)]
+        spans = [pl.ds(pl.multiple_of(b * slots, slots), slots) for b in group]
+        scores = [
+            lax.dot_general(q_rows[at, :].astype(BF16), k_buf[b], (((1,), (1,)), ((), ())), preferred_element_type=F32)
+            for b, at in zip(group, spans)
+        ]
+        packed = []
+        for b, at, score in zip(group, spans, scores):
             valid = time <= pos_ref[b]
-            scores = jnp.where(valid, scores, MASK_FILL)
-            top = jnp.max(scores, axis=-1, keepdims=True)
-            weights = jnp.where(valid, jnp.exp(scores - top), 0.0)
+            score = jnp.where(valid, score * scale, MASK_FILL)
+            top = jnp.max(score, axis=-1, keepdims=True)
+            weights = jnp.where(valid, jnp.exp(score - top), 0.0)
             total = jnp.sum(weights, axis=-1, keepdims=True)
-            num_rows[at, :] = jnp.dot(weights.astype(BF16), v_buf[b], preferred_element_type=F32)
             max_rows[at, :] = jnp.broadcast_to(top, (slots, LANES))
             sum_rows[at, :] = jnp.broadcast_to(total, (slots, LANES))
+            packed.append(weights.astype(BF16))
+        nums = [jnp.dot(w, v_buf[b], preferred_element_type=F32) for b, w in zip(group, packed)]
+        for at, num in zip(spans, nums):
+            num_rows[at, :] = num
 
     lane = lax.broadcasted_iota(jnp.int32, (rows, LANES), 1)
     width = group_size * head_dim
@@ -455,7 +487,6 @@
     hbm_spec = pl.BlockSpec(memory_space=pltpu.HBM)
     vmem_spec = pl.BlockSpec(memory_space=pltpu.VMEM)
     smem_spec = pl.BlockSpec(memory_space=pltpu.SMEM)
-    kv_width = w_k.shape[1]
     row_buf = pltpu.VMEM((rows * slots, LANES), F32)
     new_buf = pltpu.VMEM((rows * kv_local, head_dim), F32)
     return pl.pallas_call(
@@ -464,8 +495,8 @@
             jax.ShapeDtypeStruct((kv_local, rows, group_size * head_dim + LANES), F32),
             jax.ShapeDtypeStruct(k_flat.shape, BF16),
             jax.ShapeDtypeStruct(v_flat.shape, BF16),
-            jax.ShapeDtypeStruct((rows, kv_width), BF16),
-            jax.ShapeDtypeStruct((rows, kv_width), BF16),
+            jax.ShapeDtypeStruct((rows * kv_local, head_dim), BF16),
+            jax.ShapeDtypeStruct((rows * kv_local, head_dim), BF16),
         ),
         in_specs=[vmem_spec] * 4 + [smem_spec] + [hbm_spec] * 5,
         out_specs=(vmem_spec, hbm_spec, hbm_spec, vmem_spec, vmem_spec),
@@ -480,12 +511,12 @@
             pltpu.SemaphoreType.DMA((w_q.shape[1] // (2 * head_dim) + 4,)),
             pltpu.SemaphoreType.DMA((2,)),
         ],
-        compiler_params=pltpu.CompilerParams(vmem_limit_bytes=56 * 1024 * 1024),
+        compiler_params=pltpu.CompilerParams(vmem_limit_bytes=60 * 1024 * 1024),
         name="front_of_layer",
     )(x_in, gain, cos_part, sin_part, positions, w_q, w_k, w_v, k_flat, v_flat)
 
 
-def rest_of_layer(mesh, parts, own_x, gain, w_o, w_gate, w_up, w_down):
+def rest_of_layer(mesh, parts, own_x, gains, w_o, w_gate, w_up, w_down):
     nx, ny = mesh.shape["sp"] // CORES, mesh.shape["tp"]
     dim = w_o.shape[1]
     half = dim // CORES
@@ -496,14 +527,13 @@
     vmem_spec = pl.BlockSpec(memory_space=pltpu.VMEM)
     width = heads_width + LANES
     chunk_rows = ny * SUBROWS
-    count = 152
+    count = 226
     scratch = [
-        pltpu.VMEM((SUBROWS, half), BF16),
         pltpu.VMEM((w_o.shape[0], half), BF16),
         pltpu.VMEM(w_gate.shape, BF16),
         pltpu.VMEM(w_up.shape, BF16),
         pltpu.VMEM(w_down.shape, BF16),
-        pltpu.SemaphoreType.DMA((5,)),
+        pltpu.SemaphoreType.DMA((4,)),
         pltpu.VMEM((nx, chunk_rows, width), F32),
         pltpu.VMEM((nx, chunk_rows, width), F32),
         pltpu.VMEM((6, chunk_rows // 2, width), F32),
@@ -517,7 +547,7 @@
         pltpu.VMEM((nx, ny, SUBROWS, half), F32),
         pltpu.VMEM((nx, ny, SUBROWS, half), F32),
         pltpu.VMEM((nx, ny, SUBROWS, half), F32),
-        pltpu.VMEM((2, 6, nx, SUBROWS, eighth), F32),
+        pltpu.VMEM((2, nx, 6, SUBROWS, eighth), F32),
         pltpu.VMEM((2, 6, SUBROWS, eighth), F32),
         pltpu.VMEM((CORES, nx, ny, SUBROWS, half), F32),
         pltpu.SemaphoreType.DMA((count,)),
@@ -526,12 +556,12 @@
     return pl.pallas_call(
         functools.partial(rest_kernel, nx, ny, dim),
         out_shape=jax.ShapeDtypeStruct((rows, dim), BF16),
-        in_specs=[vmem_spec] * 2 + [any_spec] * 5,
+        in_specs=[vmem_spec] * 3 + [any_spec] * 4,
         out_specs=vmem_spec,
         scratch_shapes=scratch,
-        compiler_params=pltpu.CompilerParams(collective_id=0, has_side_effects=True, vmem_limit_bytes=60 * 1024 * 1024),
+        compiler_params=pltpu.CompilerParams(collective_id=0, has_side_effects=True, vmem_limit_bytes=50 * 1024 * 1024),
         name="rest_of_layer",
-    )(parts, gain, own_x, w_o, w_gate, w_up, w_down)
+    )(parts, gains, own_x, w_o, w_gate, w_up, w_down)
 
 
 def solution(mesh):
@@ -545,19 +575,18 @@
     def local_step(x_in, positions, k_cache, v_cache, attn_gain, w_q, w_k, w_v, w_o, mlp_gain, w_gate, w_up, w_down):
         num_rows, block_len, kv_local, head_dim = k_cache.shape
         dim = x_in.shape[1]
-        half = dim // CORES
+        gains = jnp.stack([attn_gain, mlp_gain]).astype(F32)
         cos_part, sin_part = rotary_tables(positions, head_dim)
         flat = (num_rows, block_len * kv_local, head_dim)
         parts, k_out, v_out, k_new, v_new = front_of_layer(
-            x_in, attn_gain.astype(F32)[None, :], cos_part, sin_part, positions, w_q, w_k, w_v,
+            x_in, gains, cos_part, sin_part, positions, w_q, w_k, w_v,
             k_cache.reshape(flat), v_cache.reshape(flat), kv_local,
         )
         k_out, v_out = k_out.reshape(k_cache.shape), v_out.reshape(v_cache.shape)
         k_new, v_new = k_new.reshape(num_rows, kv_local, head_dim), v_new.reshape(num_rows, kv_local, head_dim)
         parts = parts.reshape(kv_local, nx, num_rows // nx, parts.shape[-1])
         own_x = x_in.reshape(nx * ny, SUBROWS, dim)
-        gain = mlp_gain.astype(F32).reshape(CORES, 1, half)
-        x_out = rest_of_layer(mesh, parts, own_x, gain, w_o, w_gate, w_up, w_down)
+        x_out = rest_of_layer(mesh, parts, own_x, gains, w_o, w_gate, w_up, w_down)
         return x_out, k_out, v_out, k_new, v_new
 
     return jax.shard_map(local_step, mesh=mesh, in_specs=in_specs, out_specs=out_specs, check_vma=False)

time: 149 us -> 114 us (0.77)
  Pallas kernels: 138 us -> 107 us
  other arithmetic: 4.36 us -> 2.41 us
  local copies, waits for them, and re-layouts: 5.67 us -> 3.78 us
    pallas_call x1, Pallas kernels: 48.9 us -> 22.1 us  [front_of_layer(): pl.pallas_call(functools.partial(front_kernel, group_size, kv_local), out...]
    pallas_call x1, Pallas kernels: 88.8 us -> 85.1 us  [rest_of_layer(): pl.pallas_call(functools.partial(rest_kernel, nx, ny, dim), out_shape=jax...]
    reshape x2 -> x0, local copies, waits for them, and re-layouts: 2.98 us -> none  [the longest x1 1.49 us: local_step(): k_new.reshape(num_rows, kv_local, head_dim)]
where the time goes in v3:
time: 114 us
  Pallas kernels  107 us (94%)
  local copies, waits for them, and re-layouts  3.78 us (3%)
  other arithmetic  2.41 us (2%)
    pallas_call x1, Pallas kernels, rest_of_layer(): pl.pallas_call(functools.partial(rest_kernel, nx, ny, dim), out_shape=jax...  85.1 us
    pallas_call x1, Pallas kernels, front_of_layer(): pl.pallas_call(functools.partial(front_kernel, group_size, kv_local), out...  22.1 us
    unnamed x7, local copies, waits for them, and re-layouts  2.33 us

profile of v3, /device:TPU:97, one launch (start us, length us, event | category | flops | bytes accessed | tf_op | source)
XLA Modules:
  0.0 114.0 jit_solution(989502228387769208)
XLA Ops:
  0.6 0.7 convert_element_type.7
  1.3 0.7 stack.9
  2.0 0.7 stack.10
  2.8 0.7 maximum_convert_fusion.gain_ref
  3.4 0.3 fusion
  3.8 0.8 pad_maximum_fusion
  4.5 0.0 copy-start
  4.5 0.0 copy-start.2
  4.5 22.1 %front_of_layer.1 = (f32[2,128,896]{2,1,0:T(8,128)}, bf16[128,128,128]{2,1,0:T(8,128)(2,1)}, bf16[128,128,128]{2,1,0:T(8,128)(2,1)}, bf16[256,128]{1,0:T(8,128)(2,1)}, bf16[256,128]{1,0:T(8,128)(2,1)}) custom-call(bf16[128,6144]{1,0:T(8,128)(2,1)} %x_ref.1, f32[2,6144]{1,0:T(2,128)} %maximum_convert_fusion.gain_ref, f32[128,128]{1,0:T(8,128)} %get-tuple-element.18.cos_ref, ...), custom_call_target="tpu_custom_call" | custom-call | tf_op jit(solution)/shard_map/front_of_layer/pallas_call | solution.py:492
  26.6 0.0 copy-done
  26.6 0.0 copy-done.2
  26.6 0.0 copy-start.1
  26.6 1.2 %copy-done.1 = f32[2,128,896]{2,1,0:T(8,128)S(1)} copy-done((f32[2,128,896]{2,1,0:T(8,128)S(1)}, f32[2,128,896]{2,1,0:T(8,128)}, u32[]{:S(2)}) %copy-start.1) | copy-done | bytes 917528
  27.8 85.1 %rest_of_layer.1 = bf16[128,6144]{1,0:T(8,128)(2,1)S(1)} custom-call(f32[2,4,32,896]{3,2,1,0:T(8,128)S(1)} %bitcast.9, f32[2,6144]{1,0:T(2,128)S(1)} %copy-done.2, bf16[16,8,6144]{2,1,0:T(8,128)(2,1)S(1)} %bitcast.8, bf16[1536,6144]{1,0:T(8,128)(2,1)} %wo_hbm.1, bf16[6144,512]{1,0:T(8,128)(2,1)} %w1_hbm.1, bf16[6144,512]{1,0:T(8,128)(2,1)} %w3_hbm.1, ...), custom_call_target="tpu_custom_call" | custom-call | tf_op jit(solution)/shard_map/rest_of_layer/pallas_call | solution.py:556
  112.9 1.1 %copy.19 = bf16[128,6144]{1,0:T(8,128)(2,1)} copy(bf16[128,6144]{1,0:T(8,128)(2,1)S(1)} %rest_of_layer.1) | data formatting | bytes 3145728
  (1 shorter events, 0.0 us)
Async XLA Ops:
  4.5 22.1 %copy-start = (bf16[128,6144]{1,0:T(8,128)(2,1)S(1)}, bf16[128,6144]{1,0:T(8,128)(2,1)}, u32[]{:S(2)}) copy-start(bf16[128,6144]{1,0:T(8,128)(2,1)} %x_ref.1) | copy-start | bytes 4718596
  4.5 22.1 %copy-start.2 = (f32[2,6144]{1,0:T(2,128)S(1)}, f32[2,6144]{1,0:T(2,128)}, u32[]{:S(2)}) copy-start(f32[2,6144]{1,0:T(2,128)} %maximum_convert_fusion.gain_ref) | copy-start | bytes 147460
  26.6 1.2 %copy-start.1 = (f32[2,128,896]{2,1,0:T(8,128)S(1)}, f32[2,128,896]{2,1,0:T(8,128)}, u32[]{:S(2)}) copy-start(f32[2,128,896]{2,1,0:T(8,128)} %get-tuple-element.10) | copy-start | bytes 2752516

commit v4 on v3

--- a/solution.py
+++ b/solution.py
@@ -24,7 +24,7 @@
     inv_freq = ROPE_THETA ** (jnp.arange(half_dim, dtype=F32) * (-2.0 / head_dim))
     angles = positions.astype(F32)[:, None] * inv_freq[None, :]
     cos_part, sin_part = jnp.cos(angles), jnp.sin(angles)
-    return jnp.concatenate([cos_part, cos_part], axis=-1), jnp.concatenate([-sin_part, sin_part], axis=-1)
+    return cos_part, sin_part
 
 
 def run_together(*flows):
@@ -175,7 +175,7 @@
         return proj.at[t, :, pl.ds(h * (half // 2), half // 2)]
 
     reduce_all(proj_piece, proj_in, on_ring_y, add_into)
-    x_mid = (x_ref[ix * ny + iy, :, my_cols].astype(F32) + proj[iy]).astype(BF16).astype(F32)
+    x_mid = (x_ref[...] + proj[iy]).astype(BF16).astype(F32)
 
     square = jnp.sum(x_mid * x_mid, axis=-1, keepdims=True)
     stat_out[...] = jnp.broadcast_to(square, stat_out.shape)
@@ -184,15 +184,31 @@
     inv_rms = lax.rsqrt((stat_out[:, :1] + stat_in[:, :1]) / dim + NORM_EPS)
     gathered[core, ix, iy] = (x_mid * inv_rms * gain_ref[1:2, my_cols]).astype(BF16).astype(F32)
 
-    quarter, eighth = half // 2, half // 4
-
-    def portion(buf, lo, x_first):
+    quarter = half // 2
+
+    def either(for_one, for_zero):
+        return core * for_one + (1 - core) * for_zero
+
+    def ring_of(step_x, step_y):
+        def at(step):
+            return step_x * on_x(step) + step_y * on_y(step)
+
+        def peer(step):
+            to_x = step_x * on_x(step) + (1 - step_x) * ix
+            to_y = step_y * on_y(step) + (1 - step_y) * iy
+            return {"sp": to_x * CORES + core, "tp": to_y}
+
+        return at, peer(1), peer(-1)
+
+    own_ring, other_ring = ring_of(core, 1 - core), ring_of(1 - core, core)
+
+    def cells(buf, core_first):
         def cell(first, second, h=None):
-            cols = pl.ds(lo, quarter) if h is None else pl.ds(lo + h * eighth, eighth)
-            at = (first, second) if x_first else (second, first)
-            return buf.at[(*at, slice(None), cols)]
-
-        return cell, (on_ring_x, on_ring_y) if x_first else (on_ring_y, on_ring_x)
+            cols = slice(None) if h is None else pl.ds(h * quarter, quarter)
+            a, b = (first, second) if core_first else (second, first)
+            return buf.at[either(a, b), either(b, a), :, cols]
+
+        return cell
 
     def gather_all(buf):
         forwards = []
@@ -202,8 +218,8 @@
 
         forward(buf.at[core, ix, iy])
 
-        def flow(lo, x_first):
-            cell, (first, second) = portion(buf.at[core], lo, x_first)
+        def flow():
+            cell, first, second = cells(buf.at[core], True), own_ring, other_ring
             (f_at, f_right, f_left), (s_at, s_right, s_left) = first, second
             me = s_at(0)
 
@@ -256,7 +272,7 @@
             yield
             second_end(f_at(2), from_far)
 
-        run_together(flow(0, False), flow(quarter, True))
+        run_together(flow())
         for copy in forwards:
             copy.wait_recv()
 
@@ -288,16 +304,16 @@
         other[:, :, :, cols] = down(1 - core, j)
         swaps.append(send(other.at[:, :, :, cols], other_in.at[:, :, :, cols], partner))
 
-    def reduce_flow(index):
-        for j in range(index * tiles // 2, (index + 1) * tiles // 2):
+    def reduce_flow():
+        for j in range(tiles):
             cols = slice(j * TILE, (j + 1) * TILE)
             swaps[j].wait_recv()
             mine[:, :, :, cols] = down(core, j) + other_in[:, :, :, cols]
-        cell, (first, second) = portion(mine, index * quarter, index == 0)
+        cell, first, second = cells(mine, False), other_ring, own_ring
         here, there = first[0](0), second[0]
 
         def begin(k, t):
-            return reduce_begin(lambda to, h: cell(to, t, h), big_in.at[index, k], first, add_into)
+            return reduce_begin(lambda to, h: cell(to, t, h), big_in.at[k], first, add_into)
 
         order = (there(2), there(1), there(-1), there(0))
         states = [begin(k, order[k]) for k in range(2)]
@@ -310,7 +326,7 @@
         yield
         reduce_turn(states[2])
         reduce_end(states[0])
-        held = small_in.at[index]
+        held = small_in
         _, right, left = second
 
         def piece(t, h):
@@ -331,7 +347,7 @@
         reduce_end(states[3])
         reduce_end(last)
 
-    run_together(reduce_flow(0), reduce_flow(1))
+    run_together(reduce_flow())
     final[core, ix, iy] = (x_mid + mine[ix, iy]).astype(BF16).astype(F32)
     gather_all(final)
     for c in range(CORES):
@@ -341,13 +357,16 @@
 
 
 def front_kernel(
-    group_size, kv_local,
+    group_size, kv_local, ny,
     x_ref, gain_ref, cos_ref, sin_ref, pos_ref, wq_hbm, wk_hbm, wv_hbm, k_hbm, v_hbm,
-    parts_ref, k_out_hbm, v_out_hbm, k_new_ref, v_new_ref,
-    wq_v, wk_v, wv_v, k_buf, v_buf, normed, q_rows, num_rows, max_rows, sum_rows, k_rows, v_rows,
+    parts_ref, k_out_hbm, v_out_hbm, k_new_ref, v_new_ref, own_x_ref,
+    wq_v, wk_v, wv_v, k_buf, v_buf, normed, q_rows, num_rows, max_rows, sum_rows, k_rows, v_rows, cos_all, sin_all,
     load_sem, store_sem,
 ):
-    rows, dim = x_ref.shape
+    rows, dim = normed.shape
+    sp = lax.axis_index("sp")
+    own_cols = pl.ds(pl.multiple_of(lax.rem(sp, CORES) * (dim // CORES), dim // CORES), dim // CORES)
+    own_x_ref[...] = x_ref[sp // CORES * ny + lax.axis_index("tp"), :, own_cols].astype(F32)
     columns = k_buf.shape[1]
     block_len = columns // kv_local
     head_dim = k_buf.shape[2]
@@ -379,13 +398,16 @@
     @pl.loop(0, rows // block)
     def _(i):
         at = pl.ds(pl.multiple_of(i * block, block), block)
-        vals = x_ref[at, :].astype(F32)
+        vals = x_ref[pl.ds(i * (block // SUBROWS), block // SUBROWS)].astype(F32).reshape(block, dim)
         inv_rms = lax.rsqrt(jnp.mean(vals * vals, axis=-1, keepdims=True) + NORM_EPS)
         normed[at, :] = (vals * inv_rms * gain_ref[:1, :]).astype(BF16)
 
+    cos_all[...] = jnp.concatenate([cos_ref[...], cos_ref[...]], axis=-1)
+    sin_all[...] = jnp.concatenate([-sin_ref[...], sin_ref[...]], axis=-1)
+
     def rotate(vals):
         vals = vals.astype(BF16).astype(F32)
-        return (vals * cos_ref[...] + pltpu.roll(vals, head_dim // 2, 1) * sin_ref[...]).astype(BF16)
+        return (vals * cos_all[...] + pltpu.roll(vals, head_dim // 2, 1) * sin_all[...]).astype(BF16)
 
     wk_load.wait()
     k_proj = jnp.dot(normed[...], wk_v[...], preferred_element_type=F32)
@@ -478,8 +500,8 @@
         store.wait()
 
 
-def front_of_layer(x_in, gain, cos_part, sin_part, positions, w_q, w_k, w_v, k_flat, v_flat, kv_local):
-    rows, dim = x_in.shape
+def front_of_layer(x_in, gain, cos_part, sin_part, positions, w_q, w_k, w_v, k_flat, v_flat, kv_local, ny):
+    rows, dim = x_in.shape[0] * x_in.shape[1], x_in.shape[2]
     columns, head_dim = k_flat.shape[1:]
     group_size = w_q.shape[1] // head_dim // kv_local
     assert group_size <= SUBROWS
@@ -490,24 +512,27 @@
     row_buf = pltpu.VMEM((rows * slots, LANES), F32)
     new_buf = pltpu.VMEM((rows * kv_local, head_dim), F32)
     return pl.pallas_call(
-        functools.partial(front_kernel, group_size, kv_local),
+        functools.partial(front_kernel, group_size, kv_local, ny),
         out_shape=(
             jax.ShapeDtypeStruct((kv_local, rows, group_size * head_dim + LANES), F32),
             jax.ShapeDtypeStruct(k_flat.shape, BF16),
             jax.ShapeDtypeStruct(v_flat.shape, BF16),
             jax.ShapeDtypeStruct((rows * kv_local, head_dim), BF16),
             jax.ShapeDtypeStruct((rows * kv_local, head_dim), BF16),
+            jax.ShapeDtypeStruct((SUBROWS, dim // CORES), F32),
         ),
         in_specs=[vmem_spec] * 4 + [smem_spec] + [hbm_spec] * 5,
-        out_specs=(vmem_spec, hbm_spec, hbm_spec, vmem_spec, vmem_spec),
+        out_specs=(vmem_spec, hbm_spec, hbm_spec, vmem_spec, vmem_spec, vmem_spec),
         scratch_shapes=[
             pltpu.VMEM(w_q.shape, BF16),
             pltpu.VMEM(w_k.shape, BF16),
             pltpu.VMEM(w_v.shape, BF16),
             pltpu.VMEM(k_flat.shape, BF16),
             pltpu.VMEM(v_flat.shape, BF16),
-            pltpu.VMEM(x_in.shape, BF16),
+            pltpu.VMEM((rows, dim), BF16),
             row_buf, row_buf, row_buf, row_buf, new_buf, new_buf,
+            pltpu.VMEM((rows, head_dim), F32),
+            pltpu.VMEM((rows, head_dim), F32),
             pltpu.SemaphoreType.DMA((w_q.shape[1] // (2 * head_dim) + 4,)),
             pltpu.SemaphoreType.DMA((2,)),
         ],
@@ -522,12 +547,11 @@
     half = dim // CORES
     rows = nx * ny * SUBROWS
     heads_width = parts.shape[-1] - LANES
-    eighth = half // 4
     any_spec = pl.BlockSpec(memory_space=pltpu.HBM)
     vmem_spec = pl.BlockSpec(memory_space=pltpu.VMEM)
     width = heads_width + LANES
     chunk_rows = ny * SUBROWS
-    count = 226
+    count = 126
     scratch = [
         pltpu.VMEM((w_o.shape[0], half), BF16),
         pltpu.VMEM(w_gate.shape, BF16),
@@ -547,8 +571,8 @@
         pltpu.VMEM((nx, ny, SUBROWS, half), F32),
         pltpu.VMEM((nx, ny, SUBROWS, half), F32),
         pltpu.VMEM((nx, ny, SUBROWS, half), F32),
-        pltpu.VMEM((2, nx, 6, SUBROWS, eighth), F32),
-        pltpu.VMEM((2, 6, SUBROWS, eighth), F32),
+        pltpu.VMEM((nx, 6, SUBROWS, half // 2), F32),
+        pltpu.VMEM((6, SUBROWS, half // 2), F32),
         pltpu.VMEM((CORES, nx, ny, SUBROWS, half), F32),
         pltpu.SemaphoreType.DMA((count,)),
         pltpu.SemaphoreType.DMA((count,)),
@@ -578,14 +602,13 @@
         gains = jnp.stack([attn_gain, mlp_gain]).astype(F32)
         cos_part, sin_part = rotary_tables(positions, head_dim)
         flat = (num_rows, block_len * kv_local, head_dim)
-        parts, k_out, v_out, k_new, v_new = front_of_layer(
-            x_in, gains, cos_part, sin_part, positions, w_q, w_k, w_v,
-            k_cache.reshape(flat), v_cache.reshape(flat), kv_local,
+        parts, k_out, v_out, k_new, v_new, own_x = front_of_layer(
+            x_in.reshape(nx * ny, SUBROWS, dim), gains, cos_part, sin_part, positions, w_q, w_k, w_v,
+            k_cache.reshape(flat), v_cache.reshape(flat), kv_local, ny,
         )
         k_out, v_out = k_out.reshape(k_cache.shape), v_out.reshape(v_cache.shape)
         k_new, v_new = k_new.reshape(num_rows, kv_local, head_dim), v_new.reshape(num_rows, kv_local, head_dim)
         parts = parts.reshape(kv_local, nx, num_rows // nx, parts.shape[-1])
-        own_x = x_in.reshape(nx * ny, SUBROWS, dim)
         x_out = rest_of_layer(mesh, parts, own_x, gains, w_o, w_gate, w_up, w_down)
         return x_out, k_out, v_out, k_new, v_new
 

time: 114 us -> 117 us (1.026)
  Pallas kernels: 107 us -> 110 us
    pallas_call x1, Pallas kernels: 85.1 us -> 87.6 us  [rest_of_layer(): pl.pallas_call(functools.partial(rest_kernel, nx, ny, dim), out_shape=jax...]
where the time goes in v4:
time: 117 us
  Pallas kernels  110 us (94%)
  local copies, waits for them, and re-layouts  4.67 us (4%)
  other arithmetic  2.31 us (2%)
    pallas_call x1, Pallas kernels, rest_of_layer(): pl.pallas_call(functools.partial(rest_kernel, nx, ny, dim), out_shape=jax...  87.6 us
    pallas_call x1, Pallas kernels, front_of_layer(): pl.pallas_call(functools.partial(front_kernel, group_size, kv_local, ny),...  22 us
    unnamed x7, local copies, waits for them, and re-layouts  3.22 us

profile of v4, /device:TPU:97, one launch (start us, length us, event | category | flops | bytes accessed | tf_op | source)
XLA Modules:
  0.0 117.3 jit_solution(8261607748658292851)
XLA Ops:
  0.6 0.7 convert_element_type.7
  1.3 0.7 stack.9
  2.0 0.7 stack.10
  2.8 0.7 maximum_convert_fusion.gain_ref
  3.4 1.0 multiply_sine_fusion
  4.4 0.0 copy-start.1
  4.4 22.0 %front_of_layer.1 = (f32[2,128,896]{2,1,0:T(8,128)}, bf16[128,128,128]{2,1,0:T(8,128)(2,1)}, bf16[128,128,128]{2,1,0:T(8,128)(2,1)}, bf16[256,128]{1,0:T(8,128)(...) custom-call(bf16[16,8,6144]{2,1,0:T(8,128)(2,1)} %bitcast.11, f32[2,6144]{1,0:T(2,128)} %maximum_convert_fusion.gain_ref, ...), custom_call_target="tpu_custom_call" | custom-call | tf_op jit(solution)/shard_map/front_of_layer/pallas_call | solution.py:514
  26.4 0.0 copy-done.1
  26.4 0.0 copy-start
  26.4 1.2 copy-done
  27.6 0.0 copy-start.2
  27.6 0.9 copy-done.2
  28.5 87.6 %rest_of_layer.1 = bf16[128,6144]{1,0:T(8,128)(2,1)S(1)} custom-call(f32[2,4,32,896]{3,2,1,0:T(8,128)S(1)} %bitcast.8, f32[2,6144]{1,0:T(2,128)S(1)} %copy-done.1, f32[8,3072]{1,0:T(8,128)S(1)} %copy-done.2, bf16[1536,6144]{1,0:T(8,128)(2,1)} %wo_hbm.1, bf16[6144,512]{1,0:T(8,128)(2,1)} %w1_hbm.1, bf16[6144,512]{1,0:T(8,128)(2,1)} %w3_hbm.1, ...), custom_call_target="tpu_custom_call" | custom-call | tf_op jit(solution)/shard_map/rest_of_layer/pallas_call | solution.py:580
  116.1 1.1 copy.19
  (1 shorter events, 0.0 us)
Async XLA Ops:
  4.4 22.0 %copy-start.1 = (f32[2,6144]{1,0:T(2,128)S(1)}, f32[2,6144]{1,0:T(2,128)}, u32[]{:S(2)}) copy-start(f32[2,6144]{1,0:T(2,128)} %maximum_convert_fusion.gain_ref) | copy-start | bytes 147460
  26.4 1.2 %copy-start = (f32[2,128,896]{2,1,0:T(8,128)S(1)}, f32[2,128,896]{2,1,0:T(8,128)}, u32[]{:S(2)}) copy-start(f32[2,128,896]{2,1,0:T(8,128)} %get-tuple-element.11) | copy-start | bytes 2752516
  27.6 0.9 copy-start.2
